TPU v7x, 256 devices: a whole 4x4x8 slice. The times are simulated.
256 devices in a mesh: strip: 64 (over y, z, core), chan: 4 (over x).
Axes of the slice: x: 4, y: 4, z: 8, core: 2. Of those that a mesh axis runs over, the one named last changes fastest.
Arguments:
- activations: bfloat16 [512, 128, 1280], P('strip', None, 'chan'), may hold values from -17 to 17
- weight: bfloat16 [9, 1280, 1280], P(None, None, 'chan'), may hold values from -0.0546875 to 0.0546875
- gamma: float32 [1280], replicated, may hold values from 0.25 to 1.75
- beta: float32 [1280], replicated, may hold values from -3 to 3
- group_map: int32 [1280], replicated, may hold values from 0 to 31, as said below
- lengths: int32 [64], P('strip'), may hold values from 1 to 8, 384 in all
- stale_edges: bfloat16 [128, 128, 1280], P('strip', None, 'chan'), may hold values from -6 to 6
- stale_mean: float32 [32], replicated, may hold values from -0.5 to 0.5
- stale_square: float32 [32], replicated, may hold values from 1 to 4
- old_mean: float32 [64, 32], P('strip'), may hold values from -0.5 to 0.5
- old_square: float32 [64, 32], P('strip'), may hold values from 0.5 to 6
Outputs:
- upsampled: bfloat16 [1024, 256, 1280], P('strip', None, 'chan')
- new_mean: float32 [32], replicated
- new_square: float32 [32], replicated
Inputs may be any that keep to these rules, and one draw needn't show every extreme that they name: `group_map`: every group has exactly 40 channels. The lengths sum to 384, and some strip uses all 8 rows.
All inputs are finite; a program needn't handle non-finite values. No bound on the sum of `lengths` on one device may be relied on, other than what follows from the above.
Results may differ from a plain program's by a relative error of at most 0.0027.
Values may be sent and summed in bfloat16 or wider, within the bound.
A program may use at most 64 MiB of HBM per device.

v0:
```python
import jax
import jax.numpy as jnp
from jax import lax
from jax.sharding import PartitionSpec as P

EPS = 1e-05


def from_everyone(value, axis):
    copies = jnp.broadcast_to(value, (lax.axis_size(axis), *value.shape))
    return lax.all_to_all(copies, axis, split_axis=0, concat_axis=0, tiled=True)


def over_copies(value, axis):
    return from_everyone(value, axis).sum(axis=0)


def together(arrays, axis):
    ends = [0]
    for a in arrays:
        ends.append(ends[-1] + a.size)
    subtotal = over_copies(jnp.concatenate([a.ravel() for a in arrays]), axis)
    return tuple((subtotal[b:e].reshape(a.shape) for a, b, e in zip(arrays, ends, ends[1:])))


def padded_2(block, sides, width):
    for axis, dim in sides:
        count = lax.axis_size(axis)
        forward = [(i, i + 1) for i in range(count - 1)]
        backward = [(target, source) for source, target in forward]
        low = lax.ppermute(
            lax.slice_in_dim(block, block.shape[dim] - width, None, axis=dim), axis, forward
        )
        high = lax.ppermute(lax.slice_in_dim(block, 0, width, axis=dim), axis, backward)
        block = jnp.concatenate([low, block, high], axis=dim)
    return block


def per_device(
    activations,
    weight,
    gamma,
    beta,
    group_map,
    lengths,
    stale_edges,
    stale_mean,
    stale_square,
    old_mean,
    old_square,
):
    rows, width, local_c = activations.shape
    channels = weight.shape[1]
    groups = stale_mean.shape[0]
    per_group = channels // groups
    offset = lax.axis_index("chan") * local_c
    member = (group_map[:, None] == jnp.arange(groups, dtype=jnp.int32)[None, :]).astype(
        jnp.float32
    )
    local_member = lax.dynamic_slice_in_dim(member, offset, local_c, 0)
    length = lengths[0]
    used = (jnp.arange(rows, dtype=jnp.int32) < length).astype(jnp.float32)[:, None, None]
    values = activations.astype(jnp.float32) * used
    chan_sum = jnp.sum(values, axis=(0, 1))
    chan_sq = jnp.sum(values * values, axis=(0, 1))
    part_one = jnp.sum(chan_sum[:, None] * local_member, axis=0)
    part_two = jnp.sum(chan_sq[:, None] * local_member, axis=0)
    strip_one, strip_two = together((part_one, part_two), "chan")
    total_count = float(lax.axis_size("strip") * (3 * rows // 4) * width * per_group)
    image_one, image_two = together((strip_one, strip_two), "strip")
    new_mean = image_one / total_count
    new_square = image_two / total_count
    count = length.astype(jnp.float32) * (width * per_group)
    fresh_mean = strip_one / count
    fresh_square = strip_two / count
    mean_g = stale_mean + fresh_mean - old_mean[0]
    square_g = stale_square + fresh_square - old_square[0]
    var_g = jnp.maximum(square_g - mean_g * mean_g, 0.5 * (fresh_square - fresh_mean * fresh_mean))
    rstd_g = lax.rsqrt(var_g + EPS)
    scale_c = jnp.sum(member * rstd_g[None, :], axis=1) * gamma
    shift_c = beta - jnp.sum(member * mean_g[None, :], axis=1) * scale_c
    bordered = padded_2(stale_edges, (("strip", 0),), 1)
    bounds = jnp.stack([bordered[0], bordered[3]], axis=0)
    initial = jnp.zeros((rows * width, local_c), jnp.float32)
    total = initial
    piece = lax.all_gather(activations, "chan", axis=2, tiled=True)
    bound = lax.all_gather(bounds, "chan", axis=2, tiled=True)
    depth = piece.shape[2]
    act = (jax.nn.silu(piece.astype(jnp.float32) * scale_c + shift_c) * used).astype(jnp.bfloat16)
    padded = jnp.concatenate([bound[0:1], act, jnp.zeros((1, width, depth), jnp.bfloat16)], axis=0)
    place = (jnp.arange(rows + 2, dtype=jnp.int32) == length + 1)[:, None, None]
    padded = jnp.where(place, bound[1][None], padded)
    padded = jnp.pad(padded, ((0, 0), (1, 1), (0, 0)))
    for tap in range(9):
        down, across = (tap // 3, tap % 3)
        patch = padded[down : down + rows, across : across + width].reshape(rows * width, depth)
        total = total + jnp.dot(patch, weight[tap], preferred_element_type=jnp.float32)
    block = ((activations.astype(jnp.float32) + total.reshape(rows, width, local_c)) * used).astype(
        jnp.bfloat16
    )
    upsampled = jnp.repeat(jnp.repeat(block, 2, axis=0), 2, axis=1)
    return (upsampled, new_mean, new_square)


def solution(mesh):
    in_specs = (
        P("strip", None, "chan"),
        P(None, None, "chan"),
        P(),
        P(),
        P(),
        P("strip"),
        P("strip", None, "chan"),
        P(),
        P(),
        P("strip", None),
        P("strip", None),
    )
    out_specs = (P("strip", None, "chan"), P(), P())
    return jax.shard_map(
        per_device, mesh=mesh, in_specs=in_specs, out_specs=out_specs, check_vma=False
    )
```

profile of v0, /device:TPU:8, one launch (start us, length us, event | category | flops | bytes accessed | tf_op | source)
XLA Modules:
  0.0 104.6 jit_solution(1750470864157832420)
XLA Ops:
  7.3 2.4 %copy.58 = bf16[8,128,320]{1,0,2:T(8,128)(2,1)} copy(bf16[8,128,320]{1,2,0:T(8,128)(2,1)} %param.11) | data formatting | bytes 1310720 | tf_op args[0]
  10.4 1.4 %fusion.1 = (f32[320]{0:T(512)S(1)}, f32[320]{0:T(512)S(1)}) fusion(bf16[8,128,320]{1,2,0:T(8,128)(2,1)} %param.11, f32[8]{0:T(128)S(1)} %compare_convert_fusion), kind=kLoop, calls=%fused_computation.11 | loop fusion | flops 1637760 | bytes 657952 | tf_op jit(solution)/shard_map/reduce_sum | solution.py:64
  12.7 4.3 %all-to-all-start = ((f32[4,1,64]{2,1,0:T(1,128)}), f32[4,1,64]{2,1,0:T(1,128)S(1)}, u32[]{:S(2)}, u32[]{:S(2)}) async-start(f32[4,1,64]{2,1,0:T(1,128)} %broadcast_in_dim.46), calls=%async_computation | async-start | bytes 4096 | tf_op jit(solution)/shard_map/all_to_all | solution.py:11
  17.2 1.9 %collective-permute-start = (bf16[1,128,320]{1,0,2:T(2,128)(2,1)S(1)}, bf16[1,128,320]{1,0,2:T(2,128)(2,1)S(1)}, u32[]{:S(2)}, u32[]{:S(2)}) collective-permute-start(bf16[1,128,320]{1,0,2:T(2,128)(2,1)S(1)} %copy.65), channel_id=1, source_target_pairs={{0,4},{4,8},{8,12},{12,16},{16,20},{20,24},{24,28},{28,32},{32,36}... | collective-permute-start | bytes 245768 | tf_op jit(solution)/shard_map/ppermute | solution.py:31
  19.3 6.8 %collective-permute-start.1 = (bf16[1,128,320]{1,0,2:T(2,128)(2,1)S(1)}, bf16[1,128,320]{1,0,2:T(2,128)(2,1)S(1)}, u32[]{:S(2)}, u32[]{:S(2)}) collective-permute-start(bf16[1,128,320]{1,0,2:T(2,128)(2,1)S(1)} %copy.66), channel_id=1, source_target_pairs={{4,0},{8,4},{12,8},{16,12},{20,16},{24,20},{28,24},{32,28},{36,32}... | collective-permute-start | bytes 245768 | tf_op jit(solution)/shard_map/ppermute | solution.py:34
  26.8 10.2 %all-to-all-start.1 = ((f32[64,1,64]{2,1,0:T(1,128)}), f32[64,1,64]{2,1,0:T(1,128)S(1)}, u32[]{:S(2)}, u32[]{:S(2)}) async-start(f32[64,1,64]{2,1,0:T(1,128)} %broadcast_in_dim.50), calls=%async_computation.1 | async-start | bytes 65536 | tf_op jit(solution)/shard_map/all_to_all | solution.py:11
  37.3 8.3 %all-to-all-done.1 = f32[64,1,64]{2,1,0:T(1,128)S(1)} async-done(((f32[64,1,64]{2,1,0:T(1,128)}), f32[64,1,64]{2,1,0:T(1,128)S(1)}, u32[]{:S(2)}, u32[]{:S(2)}) %all-to-all-start.1) | async-done | bytes 16416 | tf_op jit(solution)/shard_map/all_to_all | solution.py:11
  46.6 13.9 %all_gather.6 = bf16[2,128,1280]{1,0,2:T(2,128)(2,1)S(1)} all-gather(bf16[2,128,320]{1,0,2:T(2,128)(2,1)S(1)} %pad_maximum_fusion), channel_id=1, replica_groups=mesh['strip'=64,'chan'=4] {'chan'}, dimensions={2}, use_global_device_ids=true | all-gather | bytes 819200 | tf_op jit(solution)/shard_map/all_gather | solution.py:87
  60.5 0.9 fusion.29
  62.4 3.8 %copy.59 = bf16[8,128,1280]{2,1,0:T(8,128)(2,1)S(1)} copy(bf16[8,128,1280]{1,0,2:T(8,128)(2,1)} %all-gather.2.cloned.1.call-done) | data formatting | bytes 5242880 | tf_op jit(solution)/shard_map/all_gather | solution.py:86
  66.2 1.7 %multiply_convert_fusion = bf16[8,128,1280]{2,1,0:T(8,128)(2,1)S(1)} fusion(bf16[8,128,1280]{2,1,0:T(8,128)(2,1)S(1)} %copy.59, f32[8]{0:T(128)S(1)} %compare_convert_fusion, f32[1280]{0:T(1024)S(1)} %get-tuple-element.27, f32[1280]{0:T(1024)S(1)} %get-tuple-element.28), kind=kLoop, calls=%fused_computation | loop fusion | flops 11796480 | bytes 5253152 | tf_op jit(solution)/shard_map/convert_element_type | solution.py:89
  68.3 10.1 %pad_slice_fusion = (bf16[8,128,1280]{2,1,0:T(8,128)(2,1)S(1)}, bf16[8,128,1280]{2,1,0:T(8,128)(2,1)S(1)}, bf16[8,128,1280]{2,1,0:T(8,128)(2,1)S(1)}, bf16[8,128...) fusion(bf16[10,128,1280]{2,1,0:T(8,128)(2,1)S(1)} %maximum_sele, ...), kind=kLoop, calls=%fused_computation.2 | loop fusion | bytes 34734080 | tf_op jit(solution)/shard_map/slice | solution.py:96
  78.4 2.3 %fusion.14 = f32[1024,320]{0,1:T(8,128)S(1)} fusion(bf16[1024,1280]{1,0:T(8,128)(2,1)S(1)} %bitcast.80, bf16[9,1280,320]{1,2,0:T(8,128)(2,1)} %param.12), kind=kOutput, calls=%fused_computation.32 | convolution fusion | flops 838860800 | bytes 4751360 | tf_op jit(solution)/shard_map/dot_general | solution.py:97
  80.8 2.4 %convolution_add_fusion.7 = f32[1024,320]{0,1:T(8,128)S(1)} fusion(f32[1024,320]{0,1:T(8,128)S(1)} %fusion.14, bf16[1024,1280]{1,0:T(8,128)(2,1)S(1)} %bitcast.79, bf16[9,1280,320]{1,2,0:T(8,128)(2,1)} %param.12), kind=kOutput, calls=%fused_computation.20 | convolution fusion | flops 839188480 | bytes 6062080 | tf_op jit(solution)/shard_map/dot_general | solution.py:97
  83.2 1.1 %convolution_add_fusion.6 = f32[1024,320]{0,1:T(8,128)S(1)} fusion(f32[1024,320]{0,1:T(8,128)S(1)} %convolution_add_fusion.7, bf16[1024,1280]{1,0:T(8,128)(2,1)S(1)} %bitcast.78, bf16[9,1280,320]{1,2,0:T(8,128)(2,1)S(1)} %bitcast.85), kind=kOutput, calls=%fused_computation.19 | convolution fusion | flops 839188480 | bytes 6062080 | tf_op jit(solution)/shard_map/dot_general | solution.py:97
  84.2 1.1 %convolution_add_fusion.5 = f32[1024,320]{0,1:T(8,128)S(1)} fusion(f32[1024,320]{0,1:T(8,128)S(1)} %convolution_add_fusion.6, bf16[1024,1280]{1,0:T(8,128)(2,1)S(1)} %bitcast.77, bf16[9,1280,320]{1,2,0:T(8,128)(2,1)S(1)} %bitcast.85), kind=kOutput, calls=%fused_computation.18 | convolution fusion | flops 839188480 | bytes 6062080 | tf_op jit(solution)/shard_map/dot_general | solution.py:97
  85.3 1.1 %convolution_add_fusion.4 = f32[1024,320]{0,1:T(8,128)S(1)} fusion(f32[1024,320]{0,1:T(8,128)S(1)} %convolution_add_fusion.5, bf16[1024,1280]{1,0:T(8,128)(2,1)S(1)} %bitcast.76, bf16[9,1280,320]{1,2,0:T(8,128)(2,1)S(1)} %bitcast.85), kind=kOutput, calls=%fused_computation.17 | convolution fusion | flops 839188480 | bytes 6062080 | tf_op jit(solution)/shard_map/dot_general | solution.py:97
  86.3 1.1 %convolution_add_fusion.3 = f32[1024,320]{0,1:T(8,128)S(1)} fusion(f32[1024,320]{0,1:T(8,128)S(1)} %convolution_add_fusion.4, bf16[1024,1280]{1,0:T(8,128)(2,1)S(1)} %bitcast.75, bf16[9,1280,320]{1,2,0:T(8,128)(2,1)S(1)} %bitcast.85), kind=kOutput, calls=%fused_computation.16 | convolution fusion | flops 839188480 | bytes 6062080 | tf_op jit(solution)/shard_map/dot_general | solution.py:97
  87.4 1.1 %convolution_add_fusion.2 = f32[1024,320]{0,1:T(8,128)S(1)} fusion(f32[1024,320]{0,1:T(8,128)S(1)} %convolution_add_fusion.3, bf16[1024,1280]{1,0:T(8,128)(2,1)S(1)} %bitcast.74, bf16[9,1280,320]{1,2,0:T(8,128)(2,1)S(1)} %bitcast.85), kind=kOutput, calls=%fused_computation.15 | convolution fusion | flops 839188480 | bytes 6062080 | tf_op jit(solution)/shard_map/dot_general | solution.py:97
  88.5 1.1 %convolution_add_fusion.1 = f32[1024,320]{0,1:T(8,128)S(1)} fusion(f32[1024,320]{0,1:T(8,128)S(1)} %convolution_add_fusion.2, bf16[1024,1280]{1,0:T(8,128)(2,1)S(1)} %bitcast.73, bf16[9,1280,320]{1,2,0:T(8,128)(2,1)S(1)} %bitcast.85), kind=kOutput, calls=%fused_computation.14 | convolution fusion | flops 839188480 | bytes 6062080 | tf_op jit(solution)/shard_map/dot_general | solution.py:97
  89.5 1.1 %fusion.2 = f32[40,8,8,128]{3,2,1,0:T(8,128)S(1)} fusion(f32[1024,320]{0,1:T(8,128)S(1)} %convolution_add_fusion.1, bf16[1024,1280]{1,0:T(8,128)(2,1)S(1)} %bitcast.72, bf16[9,1280,320]{1,2,0:T(8,128)(2,1)S(1)} %bitcast.85), kind=kOutput, calls=%fused_computation.13 | convolution fusion | flops 839188480 | bytes 6062080 | tf_op jit(solution)/shard_map/dot_general | solution.py:97
  91.1 1.9 %copy.62 = bf16[16,128,320]{2,0,1:T(8,128)(2,1)} copy(bf16[16,128,320]{1,2,0:T(8,128)(2,1)S(1)} %bitcast.71) | data formatting | bytes 2621440 | tf_op jit(solution)/shard_map/reshape | solution.py:101
  92.9 1.7 %broadcast_in_dim.49 = bf16[16,128,2,320]{3,0,2,1:T(8,128)(2,1)S(1)} broadcast(bf16[16,128,320]{2,0,1:T(8,128)(2,1)} %copy.62), dimensions={0,1,3} | broadcast | bytes 3932160 | tf_op jit(solution)/shard_map/broadcast_in_dim | solution.py:101
  94.6 3.1 %copy.64 = bf16[16,256,320]{1,2,0:T(8,128)(2,1)} copy(bf16[16,256,320]{2,0,1:T(8,128)(2,1)S(1)} %bitcast.70) | data formatting | bytes 5242880
  (52 shorter events, 5.0 us)
Async XLA Ops:
  7.2 4.7 %copy-start.2 = (s32[1280]{0:T(1024)S(1)}, s32[1280]{0:T(1024)}, u32[]{:S(2)}) copy-start(s32[1280]{0:T(1024)} %param.15) | copy-start | bytes 15364
  7.2 9.9 %copy-start.1 = (bf16[2,128,320]{1,2,0:T(8,128)(2,1)S(1)}, bf16[2,128,320]{1,2,0:T(8,128)(2,1)}, u32[]{:S(2)}) copy-start(bf16[2,128,320]{1,2,0:T(8,128)(2,1)} %param.17) | copy-start | bytes 491524
  7.2 29.8 %copy-start.8 = (f32[32]{0:T(128)S(1)}, f32[32]{0:T(128)}, u32[]{:S(2)}) copy-start(f32[32]{0:T(128)} %param.18) | copy-start | bytes 388
  7.2 29.8 %copy-start.6 = (f32[32]{0:T(128)S(1)}, f32[32]{0:T(128)}, u32[]{:S(2)}) copy-start(f32[32]{0:T(128)} %param.19) | copy-start | bytes 388
  7.2 29.8 %copy-start.7 = (f32[1,32]{1,0:T(1,128)S(1)}, f32[1,32]{1,0:T(1,128)}, u32[]{:S(2)}) copy-start(f32[1,32]{1,0:T(1,128)} %param.20) | copy-start | bytes 388
  7.2 29.8 %copy-start.5 = (f32[1,32]{1,0:T(1,128)S(1)}, f32[1,32]{1,0:T(1,128)}, u32[]{:S(2)}) copy-start(f32[1,32]{1,0:T(1,128)} %param.21) | copy-start | bytes 388
  7.2 30.0 %copy-start.4 = (f32[1280]{0:T(1024)S(1)}, f32[1280]{0:T(1024)}, u32[]{:S(2)}) copy-start(f32[1280]{0:T(1024)} %param.13) | copy-start | bytes 15364
  7.2 30.0 %copy-start.3 = (f32[1280]{0:T(1024)S(1)}, f32[1280]{0:T(1024)}, u32[]{:S(2)}) copy-start(f32[1280]{0:T(1024)} %param.14) | copy-start | bytes 15364
  7.2 55.1 %all-gather.2.cloned.1.call-start = ((), (), s32[]{:S(2)}) async-start(), calls=%async_computation.2 | async-start | bytes 3276800 | tf_op jit(solution)/shard_map/all_gather | solution.py:86
  12.7 13.4 %all-to-all-start = ((f32[4,1,64]{2,1,0:T(1,128)}), f32[4,1,64]{2,1,0:T(1,128)S(1)}, u32[]{:S(2)}, u32[]{:S(2)}) async-start(f32[4,1,64]{2,1,0:T(1,128)} %broadcast_in_dim.46), calls=%async_computation | async-start | bytes 4096 | tf_op jit(solution)/shard_map/all_to_all | solution.py:11
  17.2 29.0 %collective-permute-start = (bf16[1,128,320]{1,0,2:T(2,128)(2,1)S(1)}, bf16[1,128,320]{1,0,2:T(2,128)(2,1)S(1)}, u32[]{:S(2)}, u32[]{:S(2)}) collective-permute-start(bf16[1,128,320]{1,0,2:T(2,128)(2,1)S(1)} %copy.65), channel_id=1, source_target_pairs={{0,4},{4,8},{8,12},{12,16},{16,20},{20,24},{24,28},{28,32},{32,36}... | collective-permute-start | bytes 245768 | tf_op jit(solution)/shard_map/ppermute | solution.py:31
  19.3 26.9 %collective-permute-start.1 = (bf16[1,128,320]{1,0,2:T(2,128)(2,1)S(1)}, bf16[1,128,320]{1,0,2:T(2,128)(2,1)S(1)}, u32[]{:S(2)}, u32[]{:S(2)}) collective-permute-start(bf16[1,128,320]{1,0,2:T(2,128)(2,1)S(1)} %copy.66), channel_id=1, source_target_pairs={{4,0},{8,4},{12,8},{16,12},{20,16},{24,20},{28,24},{32,28},{36,32}... | collective-permute-start | bytes 245768 | tf_op jit(solution)/shard_map/ppermute | solution.py:34
  26.8 18.7 %all-to-all-start.1 = ((f32[64,1,64]{2,1,0:T(1,128)}), f32[64,1,64]{2,1,0:T(1,128)S(1)}, u32[]{:S(2)}, u32[]{:S(2)}) async-start(f32[64,1,64]{2,1,0:T(1,128)} %broadcast_in_dim.50), calls=%async_computation.1 | async-start | bytes 65536 | tf_op jit(solution)/shard_map/all_to_all | solution.py:11
  78.4 4.7 %slice-start = ((s8[7372800]{0:T(1024)(128)(4,1)}), s8[4194304]{0:T(1024)(128)(4,1)S(1)}, s32[]{:S(2)}) async-start(s8[7372800]{0:T(1024)(128)(4,1)} %bitcast.84), calls=%async_computation.3 | async-start | bytes 8388608
  80.8 2.4 %slice-start.1 = ((s8[7372800]{0:T(1024)(128)(4,1)}), s8[3178496]{0:T(1024)(128)(4,1)S(1)}, s32[]{:S(2)}) async-start(s8[7372800]{0:T(1024)(128)(4,1)} %bitcast.84), calls=%async_computation.4 | async-start | bytes 6356992
  89.5 1.1 %copy-start = (bf16[8,128,320]{1,2,0:T(8,128)(2,1)S(1)}, bf16[8,128,320]{1,2,0:T(8,128)(2,1)}, u32[]{:S(2)}) copy-start(bf16[8,128,320]{1,2,0:T(8,128)(2,1)} %param.11) | copy-start | bytes 1966084
Sparse Core Ops, SparseCore 0:
  10.4 40.5 all-gather.1
where the time goes:
time: 106 us; the launch traced here: 105 us
  local copies, waits for them, and re-layouts  26.7 us (25%)
  starting transfers between devices  23.2 us (22%)
  between operations  15.1 us (14%)
  blocking collectives  13.9 us (13%)
  matrix products  12.1 us (11%)
  waiting for transfers between devices  8.35 us (8%)
  other arithmetic  5.3 us (5%)
    all_to_all x2, starting transfers between devices, from_everyone(): return lax.all_to_all(copies, axis, split_axis=0, concat_axis=0, tiled=True)  14.4 us
    all_gather x1, blocking collectives, per_device(): bound = lax.all_gather(bounds, 'chan', axis=2, tiled=True)  13.9 us
    dot_general x9, matrix products, per_device(): jnp.dot(patch, weight[tap], preferred_element_type=jnp.float32)  12.1 us
    slice x1, local copies, waits for them, and re-layouts, per_device(): padded[down:down + rows, across:across + width].reshape(rows * width, depth)  10.1 us
    all_to_all x2, waiting for transfers between devices, from_everyone(): return lax.all_to_all(copies, axis, split_axis=0, concat_axis=0, tiled=True)  8.31 us
    ppermute x1, starting transfers between devices, padded_2(): lax.ppermute(lax.slice_in_dim(block, 0, width, axis=dim), axis, backward)  6.81 us
    unnamed x28, local copies, waits for them, and re-layouts  6.78 us
    all_gather x1, local copies, waits for them, and re-layouts, per_device(): piece = lax.all_gather(activations, 'chan', axis=2, tiled=True)  3.83 us
  transfers between devices with their start and end apart: 5, of which 1 were waited for; matrix products, arithmetic and copies ran while one was open for 6% of the time, Pallas kernels for 0%

commit v1 on v0

v1 whole, which is shorter than its diff:
```python
import functools

import jax
import jax.numpy as jnp
from jax import lax
from jax.experimental import pallas as pl
from jax.experimental.pallas import tpu as pltpu
from jax.sharding import PartitionSpec as P

EPS = 1e-05
F32 = jnp.float32
BF16 = jnp.bfloat16
MAIN = 256
REM = 64
LANES = 128
KEY = 1024


def torus(strips):
    return {64: (4, 8), 4: (1, 2)}[strips]


def silu(v):
    return v / (1.0 + jnp.exp(-v))


def exact_dot(a, b, contract):
    return lax.dot_general(
        a, b, (contract, ((), ())), precision=lax.Precision.HIGHEST, preferred_element_type=F32
    )


def main_kernel(
    rows, width, strips, chans, per_group,
    act_hbm, edge_hbm, weight_hbm, params,
    block_out, moments_out,
    araw, ebuf, raw, feats, wts, acc, affine, st_own, st_chan, st_core, st_z, st_y,
    load_sem, wt_sem, own_send, own_recv, fwd_send, fwd_recv, edge_send, edge_recv,
    stat_send, chan_recv, core_recv, z_recv, y_recv,
):
    ny, nz = torus(strips)
    pairs = rows // 2
    edge = pairs
    x = lax.axis_index("chan")
    s = lax.axis_index("strip")
    core = s % 2
    z = (s // 2) % nz
    y = s // (2 * nz)
    right, left, far = (x + 1) % chans, (x + 3) % chans, (x + 2) % chans
    above, below = (s + strips - 1) % strips, (s + 1) % strips

    def to_z(k):
        return (y * nz + (z + k) % nz) * 2 + core

    def to_y(k):
        return (((y + k) % ny) * nz + z) * 2 + core

    partner = s + 1 - 2 * core

    loads = []
    for c in range(pairs):
        copy = pltpu.make_async_copy(
            act_hbm.at[pl.ds(2 * c, 2)], araw.at[pl.ds(2 * c, 2)], load_sem.at[c]
        )
        copy.start()
        loads.append(copy)

    barrier = pltpu.get_barrier_semaphore()
    greeted = 0
    for target in (right, left, far):
        pl.semaphore_signal(barrier, inc=1, device_id={"chan": target})
        greeted += 1
    others = [partner, above, below]
    others += [to_z(k) for k in range(1, nz)] + [to_y(k) for k in range(1, ny)]
    for target in others:
        pl.semaphore_signal(barrier, inc=1, device_id={"strip": target})
        greeted += 1

    slabs = (x, left, right, far)
    for j in range(chans):
        start = slabs[j] * (MAIN + REM)
        for dy in range(3):
            for dx in range(3):
                pltpu.make_async_copy(
                    weight_hbm.at[3 * dy + dx, pl.ds(pl.multiple_of(start, REM), MAIN)],
                    wts.at[dy, j, pl.ds(dx * MAIN, MAIN)],
                    wt_sem.at[j],
                ).start()
                pltpu.make_async_copy(
                    weight_hbm.at[3 * dy + dx, pl.ds(pl.multiple_of(start + MAIN, REM), REM)],
                    wts.at[dy, j, pl.ds(3 * MAIN + dx * REM, REM)],
                    wt_sem.at[j],
                ).start()
    tail = KEY - 3 * (MAIN + REM)
    for j in range(chans):
        for dy in range(3):
            wts[dy, j, pl.ds(KEY - tail, tail)] = jnp.zeros((tail, MAIN + REM), BF16)

    lane = lax.broadcasted_iota(jnp.int32, (1, LANES), 1)
    first_half = lane < REM
    length = params[16:17, 0:LANES]

    ones = [jnp.zeros((8, LANES), F32) for _ in range(3)]
    twos = [jnp.zeros((8, LANES), F32) for _ in range(3)]

    def fold(v):
        return jnp.sum(v.reshape(width // 8, 8, LANES), axis=0)

    for c in range(pairs):
        loads[c].wait()
        raw[0, c, :, 0:MAIN] = araw[2 * c, :, 0:MAIN]
        raw[0, c, :, MAIN:2 * MAIN] = araw[2 * c + 1, :, 0:MAIN]
        rem = jnp.concatenate(
            [araw[2 * c, :, MAIN:MAIN + REM], araw[2 * c + 1, :, MAIN:MAIN + REM]], axis=1
        )
        raw[0, c, :, 2 * MAIN:2 * MAIN + LANES] = rem
        for t in range(5):
            v = raw[0, c, :, t * LANES:(t + 1) * LANES].astype(F32)
            if t < 4:
                row = (2 * c + t // 2) + jnp.zeros((1, LANES), F32)
            else:
                row = 2 * c + jnp.where(first_half, 0.0, 1.0)
            mask = jnp.where(row < length, 1.0, 0.0)
            at = t % 2 if t < 4 else 2
            ones[at] = ones[at] + fold(v) * mask
            twos[at] = twos[at] + fold(v * v) * mask
    sums = jnp.concatenate(
        [jnp.concatenate(ones, axis=1), jnp.concatenate(twos, axis=1)], axis=0
    )

    def member(slab):
        return (
            params[pl.ds(8 + slab, 1), :]
            == lax.broadcasted_iota(jnp.int32, (LANES, MAIN + LANES), 0).astype(F32)
        ).astype(F32)

    by_group = exact_dot(sums, member(x), ((1,), (1,)))
    own = jnp.concatenate(
        [
            jnp.sum(by_group[0:8], axis=0, keepdims=True),
            jnp.sum(by_group[8:16], axis=0, keepdims=True),
            jnp.zeros((6, LANES), F32),
        ],
        axis=0,
    )
    st_own[0] = own
    st_chan[x] = own

    pl.semaphore_wait(barrier, greeted)

    sends = []

    def send(src, dst, send_sem, recv_sem, target):
        copy = pltpu.make_async_remote_copy(
            src_ref=src, dst_ref=dst, send_sem=send_sem, recv_sem=recv_sem,
            device_id=target, device_id_type=pl.DeviceIdType.MESH,
        )
        copy.start()
        sends.append(copy)

    def wait_for(dst, sem):
        pltpu.make_async_copy(dst, dst, sem).wait()

    for k in range(1, chans):
        send(
            st_own.at[0], st_chan.at[x], stat_send.at[k - 1], chan_recv.at[k - 1],
            {"chan": (x + k) % chans},
        )

    def send_own(c):
        send(raw.at[0, c], raw.at[1, c], own_send.at[0, c], own_recv.at[0, c], {"chan": right})
        send(raw.at[0, c], raw.at[2, c], own_send.at[1, c], own_recv.at[1, c], {"chan": left})

    send(edge_hbm.at[0], ebuf.at[1], edge_send.at[0], edge_recv.at[1], {"strip": above})
    send(edge_hbm.at[1], ebuf.at[0], edge_send.at[1], edge_recv.at[0], {"strip": below})
    send_own(0)
    send_own(1)

    wait_for(ebuf.at[0], edge_recv.at[0])
    wait_for(ebuf.at[1], edge_recv.at[1])
    keep_upper = jnp.where(s > 0, 1.0, 0.0).astype(BF16)
    keep_lower = jnp.where(s < strips - 1, 1.0, 0.0).astype(BF16)
    raw[0, edge, :, 0:MAIN] = ebuf[0, :, 0:MAIN] * keep_upper
    raw[0, edge, :, MAIN:2 * MAIN] = ebuf[1, :, 0:MAIN] * keep_lower
    raw[0, edge, :, 2 * MAIN:2 * MAIN + LANES] = jnp.concatenate(
        [ebuf[0, :, MAIN:MAIN + REM] * keep_upper, ebuf[1, :, MAIN:MAIN + REM] * keep_lower], axis=1
    )

    for k in range(1, chans):
        wait_for(st_chan.at[(x + chans - k) % chans], chan_recv.at[k - 1])
    strip_sum = st_chan[0]
    for k in range(1, chans):
        strip_sum = strip_sum + st_chan[k]
    st_own[1] = strip_sum
    st_core[core] = strip_sum
    count = length * float(width * per_group)
    fresh_mean = strip_sum[0:1] / count
    fresh_square = strip_sum[1:2] / count
    mean = params[12:13, 0:LANES] + fresh_mean - params[14:15, 0:LANES]
    square = params[13:14, 0:LANES] + fresh_square - params[15:16, 0:LANES]
    var = jnp.maximum(square - mean * mean, 0.5 * (fresh_square - fresh_mean * fresh_mean))
    rstd = lax.rsqrt(var + EPS)
    both = jnp.concatenate([rstd, mean, jnp.zeros((6, LANES), F32)], axis=0)
    for j in range(chans):
        spread = exact_dot(both, member(slabs[j]), ((1,), (0,)))
        scale = spread[0:1] * params[pl.ds(slabs[j], 1), :]
        shift = params[pl.ds(4 + slabs[j], 1), :] - spread[1:2] * scale
        affine[j, 0:1] = scale
        affine[j, 1:2] = shift

    send_own(edge)
    for c in range(2, pairs):
        send_own(c)
    send(
        st_own.at[1], st_core.at[core], stat_send.at[3], core_recv.at[0], {"strip": partner}
    )

    at_row = lax.broadcasted_iota(jnp.int32, (width, 1), 0)

    def shifted(a):
        before = jnp.where(at_row == 0, 0.0, pltpu.roll(a, 1, 0))
        after = jnp.where(at_row == width - 1, 0.0, pltpu.roll(a, width - 1, 0))
        return before, a, after

    def store_main(j, p, t, a):
        for dx, v in enumerate(shifted(a)):
            feats[j, p, :, dx * MAIN + t * LANES:dx * MAIN + (t + 1) * LANES] = v.astype(BF16)

    def store_rem(j, p_one, p_two, a):
        before, same, after = shifted(a)
        turned = [pltpu.roll(v, REM, 1) for v in (before, same, after)]
        base = 3 * MAIN
        feats[j, p_one, :, base:base + LANES] = jnp.where(first_half, before, turned[1]).astype(BF16)
        feats[j, p_one, :, base + LANES:base + 2 * LANES] = jnp.where(first_half, after, 0.0).astype(BF16)
        feats[j, p_two, :, base:base + LANES] = jnp.where(first_half, turned[0], same).astype(BF16)
        feats[j, p_two, :, base + LANES:base + 2 * LANES] = jnp.where(first_half, turned[2], 0.0).astype(BF16)

    def tile(j, c, t):
        return raw[j, c, :, t * LANES:(t + 1) * LANES].astype(F32)

    def prepare(j, c):
        def picked(row, t, low):
            at = t % 2 if t < 4 else 2
            lanes = slice(at * LANES, (at + 1) * LANES)
            v = tile(j, c, t) * affine[j, 0:1, lanes] + affine[j, 1:2, lanes]
            return jnp.where(row < length, silu(v), jnp.where(row == length, low, 0.0))

        first = (2 * c + jnp.zeros((1, LANES), jnp.int32)).astype(F32)
        for h in range(2):
            for t in range(2):
                a = picked(first + float(h), 2 * h + t, tile(j, edge, 2 + t))
                store_main(j, 2 * c + h + 1, t, a)
        borders = tile(j, edge, 4)
        low = jnp.where(first_half, pltpu.roll(borders, REM, 1), borders)
        store_rem(j, 2 * c + 1, 2 * c + 2, picked(first + jnp.where(first_half, 0.0, 1.0), 4, low))

    def prepare_edge(j):
        full = float(rows) == length
        for t in range(2):
            store_main(j, 0, t, tile(j, edge, t))
            store_main(j, rows + 1, t, jnp.where(full, tile(j, edge, 2 + t), 0.0))
        borders = tile(j, edge, 4)
        store_rem(j, 0, rows + 1, jnp.where(first_half | full, borders, 0.0))

    def product(j, pair, dy):
        patch = feats[j, pl.ds(2 * pair + dy, 2)].reshape(2 * width, KEY)
        return jnp.dot(patch, wts[dy, j], preferred_element_type=F32)

    def conv(j, pair, first=False):
        total = product(j, pair, 0) + product(j, pair, 1) + product(j, pair, 2)
        acc[pair] = total if first else acc[pair] + total

    def wait_weights(j):
        landed = wts.at[:, j, pl.ds(0, 3 * (MAIN + REM))]
        pltpu.make_async_copy(landed, landed, wt_sem.at[j]).wait()

    prepare_edge(0)

    @pl.loop(0, pairs)
    def _(c):
        prepare(0, c)

    wait_for(st_core.at[1 - core], core_recv.at[0])
    chip_sum = st_core[0] + st_core[1]
    st_own[2] = chip_sum
    st_z[z] = chip_sum
    wait_weights(0)

    @pl.loop(0, pairs // 2)
    def _(pair):
        conv(0, pair, first=True)

    for k in range(1, nz):
        send(st_own.at[2], st_z.at[z], stat_send.at[3 + k], z_recv.at[k - 1], {"strip": to_z(k)})

    @pl.loop(pairs // 2, pairs)
    def _(pair):
        conv(0, pair, first=True)

    def got(c):
        wait_for(raw.at[1, c], own_recv.at[0, c])
        wait_for(raw.at[2, c], own_recv.at[1, c])

    def forward(direction, c, at, half=None):
        src, dst = raw.at[1 + direction, c], raw.at[3, c]
        if half is not None:
            part = pl.ds(half * (width // 2), width // 2)
            src, dst = src.at[part], dst.at[part]
        send(
            src, dst, fwd_send.at[direction, at], fwd_recv.at[direction, at],
            {"chan": (right, left)[direction]},
        )

    def got_far(direction, c, at, half=None):
        dst = raw.at[3, c]
        if half is not None:
            dst = dst.at[pl.ds(half * (width // 2), width // 2)]
        wait_for(dst, fwd_recv.at[direction, at])

    got(0)
    got(1)
    got(edge)
    forward(0, edge, 0)
    forward(1, 1, 0)
    forward(0, 0, 1)
    wait_weights(1)
    wait_weights(2)

    @pl.loop(1, 3)
    def _(j):
        prepare_edge(j)
        prepare(j, 0)
        prepare(j, 1)
        conv(j, 0)

    for k in range(1, nz):
        wait_for(st_z.at[(z + nz - k) % nz], z_recv.at[k - 1])
    line_sum = st_z[0]
    for k in range(1, nz):
        line_sum = line_sum + st_z[k]
    st_own[3] = line_sum
    st_y[y] = line_sum
    got(2)
    forward(1, 2, 1)
    for k in range(1, ny):
        send(
            st_own.at[3], st_y.at[y], stat_send.at[2 + nz + k], y_recv.at[k - 1],
            {"strip": to_y(k)},
        )

    @pl.loop(1, 3)
    def _(j):
        prepare(j, 2)
        conv(j, 1)

    got(3)
    forward(0, 3, 2, half=0)
    forward(1, 3, 2, half=1)

    @pl.loop(1, 3)
    def _(j):
        prepare(j, 3)
        conv(j, 2)
        conv(j, 3)

    for k in range(1, ny):
        wait_for(st_y.at[(y + ny - k) % ny], y_recv.at[k - 1])
    image_sum = st_y[0]
    for k in range(1, ny):
        image_sum = image_sum + st_y[k]
    moments_out[...] = image_sum / float(strips * (3 * rows // 4) * width * per_group)

    wait_weights(3)
    got_far(0, edge, 0)
    got_far(1, 1, 0)
    prepare_edge(3)
    prepare(3, 1)
    got_far(0, 0, 1)
    got_far(1, 2, 1)

    @pl.loop(0, 2)
    def _(i):
        prepare(3, 2 * i)

    @pl.loop(0, 2)
    def _(pair):
        conv(3, pair)

    got_far(0, 3, 2, half=0)
    got_far(1, 3, 2, half=1)
    prepare(3, 3)

    @pl.loop(2, pairs)
    def _(pair):
        conv(3, pair)

    @pl.loop(0, rows)
    def _(r):
        at = (r % 2) * width
        total = acc[r // 2, pl.ds(pl.multiple_of(at, width), width)]
        value = araw[r].astype(F32) + total
        row = (r + jnp.zeros((1, 1), jnp.int32)).astype(F32)
        block_out[r] = jnp.where(row < length[:, 0:1], value, 0.0).astype(BF16)

    for copy in sends:
        copy.wait_send()


def spread_kernel(rows, width, local, block, moments, up_hbm, mean_out, square_out, buf, sem):
    twice = (
        lax.broadcasted_iota(jnp.int32, (2 * width, width), 0) // 2
        == lax.broadcasted_iota(jnp.int32, (2 * width, width), 1)
    ).astype(F32).astype(BF16)
    copies = []
    for r in range(rows):
        wide = jnp.dot(twice, block[r], preferred_element_type=F32).astype(BF16)
        buf[2 * r] = wide
        buf[2 * r + 1] = wide
        copy = pltpu.make_async_copy(
            buf.at[pl.ds(2 * r, 2)], up_hbm.at[pl.ds(2 * r, 2)], sem.at[r]
        )
        copy.start()
        copies.append(copy)
    groups = mean_out.shape[1]
    mean_out[...] = moments[0:1, 0:groups]
    square_out[...] = moments[1:2, 0:groups]
    for copy in copies:
        copy.wait()


def per_device(
    activations, weight, gamma, beta, group_map, lengths, stale_edges,
    stale_mean, stale_square, old_mean, old_square,
):
    rows, width, local = activations.shape
    channels = weight.shape[1]
    groups = stale_mean.shape[0]
    strips, chans = lax.axis_size("strip"), lax.axis_size("chan")
    ny, nz = torus(strips)
    pairs = rows // 2

    wide = MAIN + LANES

    def slabs(v):
        v = v.astype(F32).reshape(chans, local)
        return jnp.concatenate([v, v[:, MAIN:]], axis=1)

    def moment(v):
        return jnp.pad(v.reshape(1, groups), ((0, 0), (0, wide - groups)))

    params = jnp.concatenate(
        [
            slabs(gamma), slabs(beta), slabs(group_map),
            moment(stale_mean), moment(stale_square), moment(old_mean), moment(old_square),
            jnp.broadcast_to(lengths.astype(F32)[:, None], (8, wide)),
        ],
        axis=0,
    )

    dma = pltpu.SemaphoreType.DMA
    any_space = pl.BlockSpec(memory_space=pl.ANY)
    vmem = pl.BlockSpec(memory_space=pltpu.VMEM)
    flops = 2 * rows * width * 9 * channels * local
    block, moments = pl.pallas_call(
        functools.partial(main_kernel, rows, width, strips, chans, channels // groups),
        name="gather_conv",
        out_shape=(
            jax.ShapeDtypeStruct((rows, width, local), BF16),
            jax.ShapeDtypeStruct((8, LANES), F32),
        ),
        in_specs=[any_space, any_space, any_space, vmem],
        out_specs=(vmem, vmem),
        scratch_shapes=[
            pltpu.VMEM((rows, width, local), BF16),
            pltpu.VMEM((2, width, local), BF16),
            pltpu.VMEM((chans, pairs + 1, width, 2 * MAIN + LANES), BF16),
            pltpu.VMEM((chans, rows + 2, width, KEY), BF16),
            pltpu.VMEM((3, chans, KEY, local), BF16),
            pltpu.VMEM((pairs, 2 * width, local), F32),
            pltpu.VMEM((chans, 8, wide), F32),
            pltpu.VMEM((4, 8, LANES), F32),
            pltpu.VMEM((chans, 8, LANES), F32),
            pltpu.VMEM((2, 8, LANES), F32),
            pltpu.VMEM((nz, 8, LANES), F32),
            pltpu.VMEM((ny, 8, LANES), F32),
            dma((pairs,)),
            dma((chans,)),
            dma((2, pairs + 1)),
            dma((2, pairs + 1)),
            dma((2, 3)),
            dma((2, 3)),
            dma((2,)),
            dma((2,)),
            dma((3 + nz + ny,)),
            dma((chans - 1,)),
            dma((1,)),
            dma((max(nz - 1, 1),)),
            dma((max(ny - 1, 1),)),
        ],
        compiler_params=pltpu.CompilerParams(
            collective_id=0, has_side_effects=True, vmem_limit_bytes=56 * 1024 * 1024
        ),
        cost_estimate=pl.CostEstimate(
            flops=flops, bytes_accessed=weight.size * 2, transcendentals=rows * width * channels
        ),
    )(activations, stale_edges, weight, params)

    upsampled, new_mean, new_square = pl.pallas_call(
        functools.partial(spread_kernel, rows, width, local),
        name="spread",
        out_shape=(
            jax.ShapeDtypeStruct((2 * rows, 2 * width, local), BF16),
            jax.ShapeDtypeStruct((1, groups), F32),
            jax.ShapeDtypeStruct((1, groups), F32),
        ),
        in_specs=[vmem, vmem],
        out_specs=(any_space, vmem, vmem),
        scratch_shapes=[pltpu.VMEM((2 * rows, 2 * width, local), BF16), dma((rows,))],
        compiler_params=pltpu.CompilerParams(vmem_limit_bytes=32 * 1024 * 1024),
    )(block, moments)
    return upsampled, new_mean.reshape(groups), new_square.reshape(groups)


def solution(mesh):
    in_specs = (
        P("strip", None, "chan"),
        P(None, None, "chan"),
        P(),
        P(),
        P(),
        P("strip"),
        P("strip", None, "chan"),
        P(),
        P(),
        P("strip", None),
        P("strip", None),
    )
    out_specs = (P("strip", None, "chan"), P(), P())
    return jax.shard_map(
        per_device, mesh=mesh, in_specs=in_specs, out_specs=out_specs, check_vma=False
    )
```

time: 106 us -> 78.3 us (0.74)
  Pallas kernels: 0 us -> 47.8 us
  starting transfers between devices: 23.2 us -> 0 us
  blocking collectives: 13.9 us -> 0 us
  between operations: 15.1 us -> 1.31 us
  matrix products: 12.1 us -> 0 us
  waiting for transfers between devices: 8.35 us -> 0 us
  other arithmetic: 5.3 us -> 0.85 us
    pallas_call x0 -> x2, Pallas kernels: none -> 47.8 us  [the longest x1 44.1 us: per_device(): pl.pallas_call(functools.partial(main_kernel, rows, width, strips, chans,...]
    unnamed x28 -> x8, local copies, waits for them, and re-layouts: 6.78 us -> 21.4 us
    all_to_all x2 -> x0, starting transfers between devices: 14.4 us -> none  [from_everyone(): return lax.all_to_all(copies, axis, split_axis=0, concat_axis=0, tiled=True)]
    all_gather x1 -> x0, blocking collectives: 13.9 us -> none  [per_device(): bound = lax.all_gather(bounds, 'chan', axis=2, tiled=True)]
    dot_general x9 -> x0, matrix products: 12.1 us -> none  [per_device(): jnp.dot(patch, weight[tap], preferred_element_type=jnp.float32)]
    slice x3, local copies, waits for them, and re-layouts: 11 us -> 0.01 us  [slabs(): return jnp.concatenate([v, v[:, MAIN:]], axis=1)]
    ppermute x2 -> x0, starting transfers between devices: 8.73 us -> none  [the longest x1 6.81 us: padded_2(): lax.ppermute(lax.slice_in_dim(block, 0, width, axis=dim), axis, backward)]
    all_to_all x2 -> x0, waiting for transfers between devices: 8.31 us -> none  [from_everyone(): return lax.all_to_all(copies, axis, split_axis=0, concat_axis=0, tiled=True)]
  transfers between devices with their start and end apart: 5 -> 0, of which waited for: 1 -> 0; matrix products, arithmetic and copies ran while one was open for 6% -> 0% of each run, Pallas kernels for 0% -> 0%
where the time goes in v1:
time: 78.3 us; the launch traced here: 77.5 us
  Pallas kernels  47.8 us (61%)
  local copies, waits for them, and re-layouts  27.5 us (35%)
  between operations  1.31 us (2%)
  other arithmetic  0.85 us (1%)
    pallas_call x1, Pallas kernels, per_device(): pl.pallas_call(functools.partial(main_kernel, rows, width, strips, chans,...  44.1 us
    unnamed x8, local copies, waits for them, and re-layouts  21.4 us
    pallas_call x1, Pallas kernels, per_device(): pl.pallas_call(functools.partial(spread_kernel, rows, width, local), name...  3.73 us
    pad x4, local copies, waits for them, and re-layouts, moment(): return jnp.pad(v.reshape(1, groups), ((0, 0), (0, wide - groups)))  2.64 us
    concatenate x1, local copies, waits for them, and re-layouts, per_device(): jnp.concatenate([slabs(gamma), slabs(beta), slabs(group_map), moment(stal...  1.84 us
    reshape x3, local copies, waits for them, and re-layouts, slabs(): v = v.astype(F32).reshape(chans, local)  1.63 us

profile of v1, /device:TPU:8, one launch (start us, length us, event | category | flops | bytes accessed | tf_op | source)
XLA Modules:
  0.0 77.5 jit_solution(10271856425892670617)
XLA Ops:
  1.3 0.7 pad.13
  1.9 0.7 pad.14
  2.6 0.7 pad.15
  3.3 0.7 pad.16
  3.9 0.8 reshape.28
  4.7 0.8 reshape.29
  5.5 0.1 pad_maximum_fusion
  5.6 0.7 convert_element_type.11
  6.3 0.1 reshape.30
  6.3 0.1 pad_maximum_fusion.2
  6.4 1.8 %concatenate.15.params = f32[24,384]{1,0:T(8,128)} concatenate(f32[4,384]{1,0:T(4,128)S(1)} %get-tuple-element.16, f32[4,384]{1,0:T(4,128)S(1)} %get-tuple-element.17, f32[4,384]{1,0:T(4,128)S(1)} %pad_maximum_fusion.2, f32[1,384]{1,0:T(1,128)S(1)} %pad.13, f32[1,384]{1,0:T(1,128)S(1)} %pad.14, f32[1,384]{1,0:T(1,128)S(1)} %pad.15, f32[1,384]{1,0:T(1,128)S(1)} %pad.16, ...), dimensions={0} | concatenate | bytes 73728 | tf_op jit(solution)/shard_map/concatenate | solution.py:451
  8.3 1.7 %copy.15.edge_hbm = bf16[2,128,320]{2,1,0:T(8,128)(2,1)} copy(bf16[2,128,320]{1,2,0:T(8,128)(2,1)} %param.17) | data formatting | bytes 327680 | tf_op args[6]
  10.0 2.2 %copy.14.act_hbm = bf16[8,128,320]{2,1,0:T(8,128)(2,1)} copy(bf16[8,128,320]{1,2,0:T(8,128)(2,1)} %param.11) | data formatting | bytes 1310720 | tf_op args[0]
  12.2 12.9 %copy.16.weight_hbm = bf16[9,1280,320]{2,1,0:T(8,128)(2,1)} copy(bf16[9,1280,320]{1,2,0:T(8,128)(2,1)} %param.12) | data formatting | bytes 14745600 | tf_op args[1]
  25.1 44.1 %gather_conv.1 = (bf16[8,128,320]{2,1,0:T(8,128)(2,1)}, f32[8,128]{1,0:T(8,128)}) custom-call(bf16[8,128,320]{2,1,0:T(8,128)(2,1)} %copy.14.act_hbm, bf16[2,128,320]{2,1,0:T(8,128)(2,1)} %copy.15.edge_hbm, bf16[9,1280,320]{2,1,0:T(8,128)(2,1)} %copy.16.weight_hbm, f32[24,384]{1,0:T(8,128)} %concatenate.15.params), custom_call_target="tpu_custom_call" | custom-call | flops 7549747200 | bytes 7372800 | tf_op jit(solution)/shard_map/gather_conv/pallas_call | solution.py:464
  69.2 0.0 copy-start
  69.2 1.1 %copy-done = bf16[8,128,320]{2,1,0:T(8,128)(2,1)S(1)} copy-done((bf16[8,128,320]{2,1,0:T(8,128)(2,1)S(1)}, bf16[8,128,320]{2,1,0:T(8,128)(2,1)}, u32[]{:S(2)}) %copy-start) | copy-done | bytes 655384
  70.3 0.0 copy-start.1
  70.3 0.7 copy-done.1
  71.0 3.7 %spread.1 = (bf16[16,256,320]{2,1,0:T(8,128)(2,1)S(1)}, f32[1,32]{1,0:T(1,128)}, f32[1,32]{1,0:T(1,128)}) custom-call(bf16[8,128,320]{2,1,0:T(8,128)(2,1)S(1)} %copy-done, f32[8,128]{1,0:T(8,128)S(1)} %copy-done.1), custom_call_target="tpu_custom_call" | custom-call | tf_op jit(solution)/shard_map/spread/pallas_call | solution.py:508
  74.7 2.8 %copy.17 = bf16[16,256,320]{1,2,0:T(8,128)(2,1)} copy(bf16[16,256,320]{2,1,0:T(8,128)(2,1)S(1)} %get-tuple-element.13) | data formatting | bytes 5242880
  (4 shorter events, 0.0 us)
Async XLA Ops:
  69.2 1.1 %copy-start = (bf16[8,128,320]{2,1,0:T(8,128)(2,1)S(1)}, bf16[8,128,320]{2,1,0:T(8,128)(2,1)}, u32[]{:S(2)}) copy-start(bf16[8,128,320]{2,1,0:T(8,128)(2,1)} %get-tuple-element.8.block) | copy-start | bytes 1966084
  70.3 0.7 copy-start.1

commit v2 on v1

v2 whole, which is shorter than its diff:
```python
import functools

import jax
import jax.numpy as jnp
from jax import lax
from jax.experimental import pallas as pl
from jax.experimental.pallas import tpu as pltpu
from jax.sharding import PartitionSpec as P

EPS = 1e-05
F32 = jnp.float32
BF16 = jnp.bfloat16
MAIN = 256
REM = 64
SLAB = MAIN + REM
LANES = 128


def torus(strips):
    return {64: (4, 8), 4: (1, 2)}[strips]


def main_kernel(
    rows, width, strips, chans, per_group,
    act_hbm, edge_hbm, weight_hbm, gamma, beta, groups_of, lengths,
    stale_mean, stale_square, old_mean, old_square,
    block_hbm, moments_out,
    raw, feats, feats_rem, wts, wts_rem, acc, block, columns, group_col, affine,
    st_own, st_chan, st_core, st_z, st_y,
    load_sem, wt_sem, own_send, own_recv, fwd_send, fwd_recv, edge_send, edge_recv,
    stat_send, chan_recv, core_recv, z_recv, y_recv, out_sem,
):
    ny, nz = torus(strips)
    pairs = rows // 2
    tiles = chans * SLAB // LANES
    x = lax.axis_index("chan")
    s = lax.axis_index("strip")
    core = s % 2
    z = (s // 2) % nz
    y = s // (2 * nz)
    right, left, far = (x + 1) % chans, (x + 3) % chans, (x + 2) % chans
    above, below = (s + strips - 1) % strips, (s + 1) % strips
    partner = s + 1 - 2 * core
    slabs = (x, left, right, far)

    def slab_of(j):
        return (x + (j % 2) * ((7 - j) // 2) + (1 - j % 2) * (j // 2)) % chans

    def to_z(k):
        return (y * nz + (z + k) % nz) * 2 + core

    def to_y(k):
        return (((y + k) % ny) * nz + z) * 2 + core

    loads = []
    for c in range(pairs):
        copy = pltpu.make_async_copy(
            act_hbm.at[pl.ds(2 * c, 2)], raw.at[0, pl.ds(2 * c, 2)], load_sem.at[c]
        )
        copy.start()
        loads.append(copy)

    barrier = pltpu.get_barrier_semaphore()
    greeted = 0
    for target in (right, left, far):
        pl.semaphore_signal(barrier, inc=1, device_id={"chan": target})
        greeted += 1
    others = [partner, above, below]
    others += [to_z(k) for k in range(1, nz)] + [to_y(k) for k in range(1, ny)]
    for target in others:
        pl.semaphore_signal(barrier, inc=1, device_id={"strip": target})
        greeted += 1

    def main_start(slab):
        return pl.multiple_of(SLAB * slab + REM * (slab % 2), LANES)

    for j in range(chans):
        for dy in range(3):
            for dx in range(3):
                pltpu.make_async_copy(
                    weight_hbm.at[3 * dy + dx, :, pl.ds(main_start(slabs[j]), MAIN)],
                    wts.at[dy, j, :, pl.ds(dx * MAIN, MAIN)],
                    wt_sem.at[j],
                ).start()
    for g in range(2):
        first = pl.multiple_of(MAIN + 2 * SLAB * ((x // 2 + g) % 2), LANES)
        for dy in range(3):
            for dx in range(3):
                pltpu.make_async_copy(
                    weight_hbm.at[3 * dy + dx, :, pl.ds(first, LANES)],
                    wts_rem.at[dy, g, :, pl.ds(dx * LANES, LANES)],
                    wt_sem.at[chans + g],
                ).start()

    lane = lax.broadcasted_iota(jnp.int32, (1, LANES), 1)
    length = jnp.full((1, LANES), lengths[0], jnp.int32)

    columns[...] = jnp.transpose(
        jnp.concatenate(
            [
                gamma[...], beta[...], groups_of[...].astype(F32),
                jnp.zeros((LANES - 3 * tiles, LANES), F32),
            ],
            axis=0,
        )
    )
    for t in range(tiles):
        group_col[t * LANES:(t + 1) * LANES] = jnp.broadcast_to(
            columns[:, 2 * tiles + t:2 * tiles + t + 1], (LANES, LANES)
        ).astype(jnp.int32)

    for copy in loads:
        copy.wait()
    group_one = jnp.zeros((1, LANES), F32)
    group_two = jnp.zeros((1, LANES), F32)
    for i in range(SLAB // REM):
        one = jnp.zeros((REM, LANES), F32)
        two = jnp.zeros((REM, LANES), F32)
        for q in range(rows):
            v = jnp.where(q < length, raw[0, q, i * REM:(i + 1) * REM, :].astype(F32), 0.0)
            one = one + v
            two = two + v * v
        own_at = pl.ds(pl.multiple_of(SLAB * x + REM * i, REM), REM)
        member = group_col[own_at] == lane
        chan_one = jnp.sum(one, axis=1, keepdims=True)
        chan_two = jnp.sum(two, axis=1, keepdims=True)
        group_one = group_one + jnp.sum(jnp.where(member, chan_one, 0.0), axis=0, keepdims=True)
        group_two = group_two + jnp.sum(jnp.where(member, chan_two, 0.0), axis=0, keepdims=True)
    own = jnp.concatenate([group_one, group_two, jnp.zeros((6, LANES), F32)], axis=0)
    st_own[0] = own
    st_chan[x] = own

    pl.semaphore_wait(barrier, greeted)

    sends = []

    def send(src, dst, send_sem, recv_sem, target):
        copy = pltpu.make_async_remote_copy(
            src_ref=src, dst_ref=dst, send_sem=send_sem, recv_sem=recv_sem,
            device_id=target, device_id_type=pl.DeviceIdType.MESH,
        )
        copy.start()
        sends.append(copy)

    def wait_for(dst, sem):
        pltpu.make_async_copy(dst, dst, sem).wait()

    edge = pairs

    def pair_of(j, c):
        return raw.at[j, pl.ds(2 * c, 2)]

    def send_own(c):
        for d, target in enumerate((right, left)):
            send(
                pair_of(0, c), pair_of(1 + d, c), own_send.at[d, c], own_recv.at[d, c],
                {"chan": target},
            )

    for k in range(1, chans):
        send(
            st_own.at[0], st_chan.at[x], stat_send.at[k - 1], chan_recv.at[k - 1],
            {"chan": (x + k) % chans},
        )
    send(edge_hbm.at[0], raw.at[0, rows + 1], edge_send.at[0], edge_recv.at[1], {"strip": above})
    send(edge_hbm.at[1], raw.at[0, rows], edge_send.at[1], edge_recv.at[0], {"strip": below})
    send_own(0)
    send_own(1)
    wait_for(raw.at[0, rows], edge_recv.at[0])
    wait_for(raw.at[0, rows + 1], edge_recv.at[1])
    send_own(edge)
    send_own(2)
    send_own(3)

    for k in range(1, chans):
        wait_for(st_chan.at[(x + chans - k) % chans], chan_recv.at[k - 1])
    strip_sum = st_chan[0]
    for k in range(1, chans):
        strip_sum = strip_sum + st_chan[k]
    st_own[1] = strip_sum
    st_core[core] = strip_sum
    groups = stale_mean.shape[1]

    def padded(ref):
        return jnp.concatenate([ref[...], jnp.zeros((1, LANES - groups), F32)], axis=1)

    count = length.astype(F32) * float(width * per_group)
    fresh_mean = strip_sum[0:1] / count
    fresh_square = strip_sum[1:2] / count
    mean = padded(stale_mean) + fresh_mean - padded(old_mean)
    square = padded(stale_square) + fresh_square - padded(old_square)
    var = jnp.maximum(square - mean * mean, 0.5 * (fresh_square - fresh_mean * fresh_mean))
    rstd = lax.rsqrt(var + EPS)
    for t in range(tiles):
        at = slice(t * LANES, (t + 1) * LANES)
        member = group_col[at] == lane
        rstd_c = jnp.sum(jnp.where(member, rstd, 0.0), axis=1, keepdims=True)
        mean_c = jnp.sum(jnp.where(member, mean, 0.0), axis=1, keepdims=True)
        scale = rstd_c * columns[:, t:t + 1]
        shift = columns[:, tiles + t:tiles + t + 1] - mean_c * scale
        affine[0, at] = jnp.broadcast_to(0.5 * scale, (LANES, LANES))
        affine[1, at] = jnp.broadcast_to(0.5 * shift, (LANES, LANES))
    send(
        st_own.at[1], st_core.at[core], stat_send.at[3], core_recv.at[0], {"strip": partner}
    )

    is_first = lane == 0
    is_last = lane == width - 1
    top = jnp.full((1, LANES), s, jnp.int32) > 0
    bottom = jnp.full((1, LANES), s, jnp.int32) < strips - 1

    def store(j, i, p, a):
        before = jnp.where(is_first, 0.0, pltpu.roll(a, 1, 1)).astype(BF16)
        after = jnp.where(is_last, 0.0, pltpu.roll(a, width - 1, 1)).astype(BF16)
        cells = pl.ds(pl.multiple_of(p * width, LANES), width)
        if i < MAIN // REM:
            for dx, v in enumerate((before, a.astype(BF16), after)):
                feats[j, dx * MAIN + i * REM:dx * MAIN + (i + 1) * REM, cells] = v
        else:
            slab = slab_of(j)
            g = (slab // 2 + x // 2) % 2
            for dx, v in enumerate((before, a.astype(BF16), after)):
                at = pl.ds(pl.multiple_of(dx * LANES + REM * (slab % 2), REM), REM)
                feats_rem[g, at, cells] = v

    def piece(j, i):
        odd = slab_of(j) % 2
        if i < MAIN // REM:
            return REM * i + REM * odd
        return MAIN * (1 - odd)

    def at_piece(start):
        return pl.ds(pl.multiple_of(start, REM), REM)

    def prepare(j, q):
        row = jnp.zeros((1, LANES), jnp.int32) + q
        for i in range(SLAB // REM):
            start = piece(j, i)
            total = at_piece(SLAB * slab_of(j) + start)
            h = raw[j, q, at_piece(start), :].astype(F32) * affine[0, total] + affine[1, total]
            a = h + h * jnp.tanh(h)
            low = raw[j, rows + 1, at_piece(start), :].astype(F32)
            low = jnp.where((row == length) & bottom, low, 0.0)
            store(j, i, q + 1, jnp.where(row < length, a, low))

    def prepare_edge(j):
        for i in range(SLAB // REM):
            start = piece(j, i)
            high = raw[j, rows, at_piece(start), :].astype(F32)
            store(j, i, 0, jnp.where(top, high, 0.0))
            low = raw[j, rows + 1, at_piece(start), :].astype(F32)
            store(j, i, rows + 1, jnp.where((length == rows) & bottom, low, 0.0))

    def prepare_pair(j, c):
        prepare(j, 2 * c)
        prepare(j, 2 * c + 1)

    def cells_of(pair, dy):
        return pl.ds(pl.multiple_of((2 * pair + dy) * width, LANES), 2 * width)

    def term(j, pair, dy):
        return jnp.dot(wts[dy, j], feats[j, :, cells_of(pair, dy)], preferred_element_type=F32)

    def term_rem(g, pair, dy):
        return jnp.dot(
            wts_rem[dy, g], feats_rem[g, :, cells_of(pair, dy)], preferred_element_type=F32
        )

    def add_to(pair, total, first=False):
        at = pl.ds(pl.multiple_of(pair * 2 * width, LANES), 2 * width)
        acc[:, at] = total if first else acc[:, at] + total

    def conv(j, pair, first=False):
        add_to(pair, term(j, pair, 0) + term(j, pair, 1) + term(j, pair, 2), first)

    def conv_rem(g, pair):
        add_to(pair, term_rem(g, pair, 0) + term_rem(g, pair, 1) + term_rem(g, pair, 2))

    def wait_weights(j):
        pltpu.make_async_copy(wts.at[:, j], wts.at[:, j], wt_sem.at[j]).wait()

    def wait_weights_rem(g):
        pltpu.make_async_copy(wts_rem.at[:, g], wts_rem.at[:, g], wt_sem.at[chans + g]).wait()

    prepare_edge(0)

    @pl.loop(0, rows)
    def _(q):
        prepare(0, q)

    wait_for(st_core.at[1 - core], core_recv.at[0])
    chip_sum = st_core[0] + st_core[1]
    st_own[2] = chip_sum
    st_z[z] = chip_sum
    wait_weights(0)

    @pl.loop(0, pairs // 2)
    def _(pair):
        conv(0, pair, first=True)

    for k in range(1, nz):
        send(st_own.at[2], st_z.at[z], stat_send.at[3 + k], z_recv.at[k - 1], {"strip": to_z(k)})

    @pl.loop(pairs // 2, pairs)
    def _(pair):
        conv(0, pair, first=True)

    def got(c):
        for d in range(2):
            wait_for(pair_of(1 + d, c), own_recv.at[d, c])

    def forward(d, at, first, number):
        part = pl.ds(first, number)
        send(
            raw.at[1 + d, part], raw.at[3, part], fwd_send.at[d, at], fwd_recv.at[d, at],
            {"chan": (right, left)[d]},
        )

    def got_far(d, at, first, number):
        wait_for(raw.at[3, pl.ds(first, number)], fwd_recv.at[d, at])

    plan = (
        ((rows, 2), (0, 2), (6, 1)),
        ((2, 2), (4, 2), (7, 1)),
    )

    got(0)
    got(1)
    forward(1, 0, *plan[1][0])
    got(edge)
    forward(0, 0, *plan[0][0])
    forward(0, 1, *plan[0][1])
    wait_weights(1)
    wait_weights(2)

    @pl.loop(1, 3)
    def _(j):
        prepare_edge(j)
        prepare_pair(j, 0)
        prepare_pair(j, 1)
        conv(j, 0)

    for k in range(1, nz):
        wait_for(st_z.at[(z + nz - k) % nz], z_recv.at[k - 1])
    line_sum = st_z[0]
    for k in range(1, nz):
        line_sum = line_sum + st_z[k]
    st_own[3] = line_sum
    st_y[y] = line_sum
    got(2)
    forward(1, 1, *plan[1][1])
    for k in range(1, ny):
        send(
            st_own.at[3], st_y.at[y], stat_send.at[2 + nz + k], y_recv.at[k - 1],
            {"strip": to_y(k)},
        )

    @pl.loop(1, 3)
    def _(j):
        prepare_pair(j, 2)
        conv(j, 1)

    got(3)
    forward(0, 2, *plan[0][2])
    forward(1, 2, *plan[1][2])

    @pl.loop(1, 3)
    def _(j):
        prepare_pair(j, 3)
        conv(j, 2)
        conv(j, 3)

    wait_weights_rem(0)

    @pl.loop(0, pairs)
    def _(pair):
        conv_rem(0, pair)

    for k in range(1, ny):
        wait_for(st_y.at[(y + ny - k) % ny], y_recv.at[k - 1])
    image_sum = st_y[0]
    for k in range(1, ny):
        image_sum = image_sum + st_y[k]
    moments_out[...] = image_sum / float(strips * (3 * rows // 4) * width * per_group)

    wait_weights(3)
    wait_weights_rem(1)
    got_far(0, 0, *plan[0][0])
    got_far(1, 0, *plan[1][0])
    prepare_edge(3)
    prepare_pair(3, 1)
    got_far(0, 1, *plan[0][1])
    got_far(1, 1, *plan[1][1])

    outs = []

    def finish(pair):
        for h in range(2):
            r = 2 * pair + h
            value = raw[0, r].astype(F32) + acc[:, r * width:(r + 1) * width]
            block[r] = jnp.where(r < length, value, 0.0).astype(BF16)

    def put(pair):
        at = pl.ds(2 * pair, 2)
        copy = pltpu.make_async_copy(block.at[at], block_hbm.at[at], out_sem.at[pair])
        copy.start()
        outs.append(copy)

    @pl.loop(0, 2)
    def _(i):
        prepare_pair(3, 2 * i)

    @pl.loop(0, 2)
    def _(pair):
        conv(3, pair)
        conv_rem(1, pair)

    finish(0)
    finish(1)
    add_to(2, term(3, 2, 0) + term(3, 2, 1) + term_rem(1, 2, 0) + term_rem(1, 2, 1))
    put(0)
    put(1)
    got_far(0, 2, *plan[0][2])
    got_far(1, 2, *plan[1][2])
    prepare_pair(3, 3)
    add_to(2, term(3, 2, 2) + term_rem(1, 2, 2))
    finish(2)
    put(2)
    conv(3, 3)
    conv_rem(1, 3)
    finish(3)
    put(3)

    for copy in sends:
        copy.wait_send()
    for copy in outs:
        copy.wait()


def spread_kernel(
    rows, width, local, block_hbm, moments, up_hbm, mean_out, square_out, block, buf, in_sem, out_sem
):
    takes = []
    for r in range(0, rows, 2):
        at = pl.ds(r, 2)
        copy = pltpu.make_async_copy(block_hbm.at[at], block.at[at], in_sem.at[r // 2])
        copy.start()
        takes.append(copy)
    twice = (
        lax.broadcasted_iota(jnp.int32, (width, 2 * width), 1) // 2
        == lax.broadcasted_iota(jnp.int32, (width, 2 * width), 0)
    ).astype(F32).astype(BF16)
    groups = mean_out.shape[1]
    mean_out[...] = moments[0:1, 0:groups]
    square_out[...] = moments[1:2, 0:groups]
    puts = []
    for r in range(rows):
        if r % 2 == 0:
            takes[r // 2].wait()
        buf[r] = jnp.dot(block[r], twice, preferred_element_type=F32).astype(BF16)
        for a in range(2):
            copy = pltpu.make_async_copy(buf.at[r], up_hbm.at[2 * r + a], out_sem.at[2 * r + a])
            copy.start()
            puts.append(copy)
    for copy in puts:
        copy.wait()


def per_device(
    activations, weight, gamma, beta, group_map, lengths, stale_edges,
    stale_mean, stale_square, old_mean, old_square,
):
    rows, width, local = activations.shape
    channels = weight.shape[1]
    groups = stale_mean.shape[0]
    strips, chans = lax.axis_size("strip"), lax.axis_size("chan")
    ny, nz = torus(strips)
    pairs = rows // 2

    def turned(v):
        return jnp.swapaxes(v, 1, 2)

    dma = pltpu.SemaphoreType.DMA
    any_space = pl.BlockSpec(memory_space=pl.ANY)
    vmem = pl.BlockSpec(memory_space=pltpu.VMEM)
    smem = pl.BlockSpec(memory_space=pltpu.SMEM)
    flops = 2 * rows * width * 9 * channels * local
    block, moments = pl.pallas_call(
        functools.partial(main_kernel, rows, width, strips, chans, channels // groups),
        name="gather_conv",
        out_shape=(
            jax.ShapeDtypeStruct((rows, local, width), BF16),
            jax.ShapeDtypeStruct((8, LANES), F32),
        ),
        in_specs=[any_space] * 3 + [vmem] * 3 + [smem] + [vmem] * 4,
        out_specs=(any_space, vmem),
        scratch_shapes=[
            pltpu.VMEM((chans, rows + 2, local, width), BF16),
            pltpu.VMEM((chans, 3 * MAIN, (rows + 2) * width), BF16),
            pltpu.VMEM((2, 3 * LANES, (rows + 2) * width), BF16),
            pltpu.VMEM((3, chans, local, 3 * MAIN), BF16),
            pltpu.VMEM((3, 2, local, 3 * LANES), BF16),
            pltpu.VMEM((local, rows * width), F32),
            pltpu.VMEM((rows, local, width), BF16),
            pltpu.VMEM((LANES, LANES), F32),
            pltpu.VMEM((channels, LANES), jnp.int32),
            pltpu.VMEM((2, channels, LANES), F32),
            pltpu.VMEM((4, 8, LANES), F32),
            pltpu.VMEM((chans, 8, LANES), F32),
            pltpu.VMEM((2, 8, LANES), F32),
            pltpu.VMEM((nz, 8, LANES), F32),
            pltpu.VMEM((ny, 8, LANES), F32),
            dma((pairs,)),
            dma((chans + 2,)),
            dma((2, pairs + 1)),
            dma((2, pairs + 1)),
            dma((2, 3)),
            dma((2, 3)),
            dma((2,)),
            dma((2,)),
            dma((3 + nz + ny,)),
            dma((chans - 1,)),
            dma((1,)),
            dma((max(nz - 1, 1),)),
            dma((max(ny - 1, 1),)),
            dma((pairs,)),
        ],
        compiler_params=pltpu.CompilerParams(
            collective_id=0, has_side_effects=True, vmem_limit_bytes=60 * 1024 * 1024
        ),
        cost_estimate=pl.CostEstimate(
            flops=flops, bytes_accessed=weight.size * 2, transcendentals=rows * width * channels
        ),
    )(
        turned(activations), turned(stale_edges), turned(weight),
        gamma.reshape(-1, LANES), beta.reshape(-1, LANES), group_map.reshape(-1, LANES), lengths,
        stale_mean.reshape(1, groups), stale_square.reshape(1, groups), old_mean, old_square,
    )

    upsampled, new_mean, new_square = pl.pallas_call(
        functools.partial(spread_kernel, rows, width, local),
        name="spread",
        out_shape=(
            jax.ShapeDtypeStruct((2 * rows, local, 2 * width), BF16),
            jax.ShapeDtypeStruct((1, groups), F32),
            jax.ShapeDtypeStruct((1, groups), F32),
        ),
        in_specs=[any_space, vmem],
        out_specs=(any_space, vmem, vmem),
        scratch_shapes=[
            pltpu.VMEM((rows, local, width), BF16),
            pltpu.VMEM((rows, local, 2 * width), BF16),
            dma((pairs,)),
            dma((2 * rows,)),
        ],
        compiler_params=pltpu.CompilerParams(vmem_limit_bytes=60 * 1024 * 1024),
    )(block, moments)
    return turned(upsampled), new_mean.reshape(groups), new_square.reshape(groups)


def solution(mesh):
    in_specs = (
        P("strip", None, "chan"),
        P(None, None, "chan"),
        P(),
        P(),
        P(),
        P("strip"),
        P("strip", None, "chan"),
        P(),
        P(),
        P("strip", None),
        P("strip", None),
    )
    out_specs = (P("strip", None, "chan"), P(), P())
    return jax.shard_map(
        per_device, mesh=mesh, in_specs=in_specs, out_specs=out_specs, check_vma=False
    )
```

time: 78.3 us -> 48.9 us (0.62)
  local copies, waits for them, and re-layouts: 27.5 us -> 0 us
  other arithmetic: 0.85 us -> 0 us
    unnamed x8 -> x0, local copies, waits for them, and re-layouts: 21.4 us -> none
    pad x4 -> x0, local copies, waits for them, and re-layouts: 2.64 us -> none  [moment(): return jnp.pad(v.reshape(1, groups), ((0, 0), (0, wide - groups)))]
    concatenate x1 -> x0, local copies, waits for them, and re-layouts: 1.84 us -> none  [per_device(): jnp.concatenate([slabs(gamma), slabs(beta), slabs(group_map), moment(stal...]
    reshape x3 -> x0, local copies, waits for them, and re-layouts: 1.63 us -> none  [slabs(): v = v.astype(F32).reshape(chans, local)]
where the time goes in v2:
time: 48.9 us; the launch traced here: 48.7 us
  Pallas kernels  47.4 us (97%)
  between operations  1.29 us (3%)
    pallas_call x1, Pallas kernels, per_device(): pl.pallas_call(functools.partial(main_kernel, rows, width, strips, chans,...  43.4 us
    pallas_call x1, Pallas kernels, per_device(): pl.pallas_call(functools.partial(spread_kernel, rows, width, local), name...  4.04 us

profile of v2, /device:TPU:8, one launch (start us, length us, event | category | flops | bytes accessed | tf_op | source)
XLA Modules:
  0.0 48.7 jit_solution(10381188990297168319)
XLA Ops:
  1.3 43.4 %gather_conv.1 = (bf16[8,320,128]{2,1,0:T(8,128)(2,1)}, f32[8,128]{1,0:T(8,128)}) custom-call(bf16[8,320,128]{2,1,0:T(8,128)(2,1)} %bitcast.13, bf16[2,320,128]{2,1,0:T(8,128)(2,1)} %bitcast.14, bf16[9,320,1280]{2,1,0:T(8,128)(2,1)} %bitcast.11, f32[10,128]{1,0:T(8,128)} %bitcast.15, f32[10,128]{1,0:T(8,128)} %bitcast.16, s32[10,128]{1,0:T(8,128)} %bitcast.17, ...), custom_call_target="tpu_custom_call" | custom-call | flops 7549747200 | bytes 7372800 | tf_op jit(solution)/shard_map/gather_conv/pallas_call | solution.py:488
  44.7 4.0 %spread.1 = (bf16[16,320,256]{2,1,0:T(8,128)(2,1)}, f32[1,32]{1,0:T(1,128)}, f32[1,32]{1,0:T(1,128)}) custom-call(bf16[8,320,128]{2,1,0:T(8,128)(2,1)} %get-tuple-element.8.block_hbm, f32[8,128]{1,0:T(8,128)} %get-tuple-element.9.moments), custom_call_target="tpu_custom_call" | custom-call | tf_op jit(solution)/shard_map/spread/pallas_call | solution.py:540

commit v3 on v2

--- a/solution.py
+++ b/solution.py
@@ -22,14 +22,18 @@
 
 def main_kernel(
     rows, width, strips, chans, per_group,
-    act_hbm, edge_hbm, weight_hbm, gamma, beta, groups_of, lengths,
-    stale_mean, stale_square, old_mean, old_square,
-    block_hbm, moments_out,
-    raw, feats, feats_rem, wts, wts_rem, acc, block, columns, group_col, affine,
+    act_hbm, edge_hbm, weight_hbm, *rest
+):
+    (
+        gamma_hbm, beta_hbm, groups_hbm, lengths,
+        stale_mean_hbm, stale_square_hbm, old_mean_hbm, old_square_hbm,
+        block_hbm, moments_hbm,
+        gamma, beta, groups_of, stale_mean, stale_square, old_mean, old_square, moments,
+        small_sem, hop, raw, feats, feats_rem, wts, wts_rem, acc, block, columns, group_col, affine,
     st_own, st_chan, st_core, st_z, st_y,
     load_sem, wt_sem, own_send, own_recv, fwd_send, fwd_recv, edge_send, edge_recv,
     stat_send, chan_recv, core_recv, z_recv, y_recv, out_sem,
-):
+    ) = rest
     ny, nz = torus(strips)
     pairs = rows // 2
     tiles = chans * SLAB // LANES
@@ -39,8 +43,10 @@
     z = (s // 2) % nz
     y = s // (2 * nz)
     right, left, far = (x + 1) % chans, (x + 3) % chans, (x + 2) % chans
-    above, below = (s + strips - 1) % strips, (s + 1) % strips
     partner = s + 1 - 2 * core
+    z_peer = (y * nz + (z + 2 * core + nz - 1) % nz) * 2 + 1 - core
+    turns = z == core * (nz - 1)
+    peer_turns = (z + 2 * core + nz - 1) % nz == (1 - core) * (nz - 1)
     slabs = (x, left, right, far)
 
     def slab_of(j):
@@ -59,14 +65,25 @@
         )
         copy.start()
         loads.append(copy)
+
+    small = []
+    for i, (src, dst) in enumerate(
+        (
+            (gamma_hbm, gamma), (beta_hbm, beta), (groups_hbm, groups_of),
+            (stale_mean_hbm, stale_mean), (stale_square_hbm, stale_square),
+            (old_mean_hbm, old_mean), (old_square_hbm, old_square),
+        )
+    ):
+        copy = pltpu.make_async_copy(src, dst, small_sem.at[i])
+        copy.start()
+        small.append(copy)
 
     barrier = pltpu.get_barrier_semaphore()
     greeted = 0
     for target in (right, left, far):
         pl.semaphore_signal(barrier, inc=1, device_id={"chan": target})
         greeted += 1
-    others = [partner, above, below]
-    others += [to_z(k) for k in range(1, nz)] + [to_y(k) for k in range(1, ny)]
+    others = [partner, z_peer] + [to_y(k) for k in range(1, ny)]
     for target in others:
         pl.semaphore_signal(barrier, inc=1, device_id={"strip": target})
         greeted += 1
@@ -95,6 +112,8 @@
     lane = lax.broadcasted_iota(jnp.int32, (1, LANES), 1)
     length = jnp.full((1, LANES), lengths[0], jnp.int32)
 
+    for copy in small:
+        copy.wait()
     columns[...] = jnp.transpose(
         jnp.concatenate(
             [
@@ -109,8 +128,57 @@
             columns[:, 2 * tiles + t:2 * tiles + t + 1], (LANES, LANES)
         ).astype(jnp.int32)
 
+    pl.semaphore_wait(barrier, greeted)
+
+    sends = []
+
+    def send(src, dst, send_sem, recv_sem, target):
+        copy = pltpu.make_async_remote_copy(
+            src_ref=src, dst_ref=dst, send_sem=send_sem, recv_sem=recv_sem,
+            device_id=target, device_id_type=pl.DeviceIdType.MESH,
+        )
+        copy.start()
+        sends.append(copy)
+
+    def wait_for(dst, sem):
+        pltpu.make_async_copy(dst, dst, sem).wait()
+
+    edge = pairs
+
+    def pair_of(j, c):
+        return raw.at[j, pl.ds(2 * c, 2)]
+
+    def send_own(c):
+        for d, target in enumerate((right, left)):
+            send(
+                pair_of(0, c), pair_of(1 + d, c), own_send.at[d, c], own_recv.at[d, c],
+                {"chan": target},
+            )
+
     for copy in loads:
         copy.wait()
+    send_own(0)
+    send(
+        edge_hbm.at[1 - core], raw.at[0, rows + core], edge_send.at[0], edge_recv.at[0],
+        {"strip": partner},
+    )
+
+    @pl.when(peer_turns)
+    def _():
+        pltpu.make_async_remote_copy(
+            src_ref=edge_hbm.at[core], dst_ref=hop, send_sem=edge_send.at[1],
+            recv_sem=edge_recv.at[1], device_id={"strip": z_peer},
+            device_id_type=pl.DeviceIdType.MESH,
+        ).start()
+
+    @pl.when(jnp.logical_not(peer_turns))
+    def _():
+        pltpu.make_async_remote_copy(
+            src_ref=edge_hbm.at[core], dst_ref=raw.at[0, rows + 1 - core],
+            send_sem=edge_send.at[1], recv_sem=edge_recv.at[1], device_id={"strip": z_peer},
+            device_id_type=pl.DeviceIdType.MESH,
+        ).start()
+
     group_one = jnp.zeros((1, LANES), F32)
     group_two = jnp.zeros((1, LANES), F32)
     for i in range(SLAB // REM):
@@ -129,45 +197,29 @@
     own = jnp.concatenate([group_one, group_two, jnp.zeros((6, LANES), F32)], axis=0)
     st_own[0] = own
     st_chan[x] = own
-
-    pl.semaphore_wait(barrier, greeted)
-
-    sends = []
-
-    def send(src, dst, send_sem, recv_sem, target):
-        copy = pltpu.make_async_remote_copy(
-            src_ref=src, dst_ref=dst, send_sem=send_sem, recv_sem=recv_sem,
-            device_id=target, device_id_type=pl.DeviceIdType.MESH,
-        )
-        copy.start()
-        sends.append(copy)
-
-    def wait_for(dst, sem):
-        pltpu.make_async_copy(dst, dst, sem).wait()
-
-    edge = pairs
-
-    def pair_of(j, c):
-        return raw.at[j, pl.ds(2 * c, 2)]
-
-    def send_own(c):
-        for d, target in enumerate((right, left)):
-            send(
-                pair_of(0, c), pair_of(1 + d, c), own_send.at[d, c], own_recv.at[d, c],
-                {"chan": target},
-            )
-
     for k in range(1, chans):
         send(
             st_own.at[0], st_chan.at[x], stat_send.at[k - 1], chan_recv.at[k - 1],
             {"chan": (x + k) % chans},
         )
-    send(edge_hbm.at[0], raw.at[0, rows + 1], edge_send.at[0], edge_recv.at[1], {"strip": above})
-    send(edge_hbm.at[1], raw.at[0, rows], edge_send.at[1], edge_recv.at[0], {"strip": below})
-    send_own(0)
     send_own(1)
-    wait_for(raw.at[0, rows], edge_recv.at[0])
-    wait_for(raw.at[0, rows + 1], edge_recv.at[1])
+    wait_for(raw.at[0, rows + 1 - core], edge_recv.at[0])
+
+    @pl.when(turns)
+    def _():
+        wait_for(hop, edge_recv.at[1])
+        pltpu.make_async_remote_copy(
+            src_ref=hop, dst_ref=raw.at[0, rows + core], send_sem=edge_send.at[2],
+            recv_sem=edge_recv.at[2],
+            device_id={"strip": ((y + 1 + core * (ny - 2)) % ny * nz + z) * 2 + core},
+            device_id_type=pl.DeviceIdType.MESH,
+        ).start()
+        wait_for(raw.at[0, rows + core], edge_recv.at[2])
+
+    @pl.when(jnp.logical_not(turns))
+    def _():
+        wait_for(raw.at[0, rows + core], edge_recv.at[1])
+
     send_own(edge)
     send_own(2)
     send_own(3)
@@ -204,22 +256,25 @@
         st_own.at[1], st_core.at[core], stat_send.at[3], core_recv.at[0], {"strip": partner}
     )
 
-    is_first = lane == 0
-    is_last = lane == width - 1
-    top = jnp.full((1, LANES), s, jnp.int32) > 0
+    def flag(condition):
+        return jnp.where(condition, 1.0, 0.0).astype(BF16)
+
+    not_first = flag(lane != 0)
+    not_last = flag(lane != width - 1)
+    top = flag(jnp.full((1, LANES), s, jnp.int32) > 0)
     bottom = jnp.full((1, LANES), s, jnp.int32) < strips - 1
 
     def store(j, i, p, a):
-        before = jnp.where(is_first, 0.0, pltpu.roll(a, 1, 1)).astype(BF16)
-        after = jnp.where(is_last, 0.0, pltpu.roll(a, width - 1, 1)).astype(BF16)
+        before = pltpu.roll(a, 1, 1) * not_first
+        after = pltpu.roll(a, width - 1, 1) * not_last
         cells = pl.ds(pl.multiple_of(p * width, LANES), width)
         if i < MAIN // REM:
-            for dx, v in enumerate((before, a.astype(BF16), after)):
+            for dx, v in enumerate((before, a, after)):
                 feats[j, dx * MAIN + i * REM:dx * MAIN + (i + 1) * REM, cells] = v
         else:
             slab = slab_of(j)
             g = (slab // 2 + x // 2) % 2
-            for dx, v in enumerate((before, a.astype(BF16), after)):
+            for dx, v in enumerate((before, a, after)):
                 at = pl.ds(pl.multiple_of(dx * LANES + REM * (slab % 2), REM), REM)
                 feats_rem[g, at, cells] = v
 
@@ -234,22 +289,21 @@
 
     def prepare(j, q):
         row = jnp.zeros((1, LANES), jnp.int32) + q
+        in_use = flag(row < length)
+        border = flag((row == length) & bottom)
         for i in range(SLAB // REM):
             start = piece(j, i)
             total = at_piece(SLAB * slab_of(j) + start)
             h = raw[j, q, at_piece(start), :].astype(F32) * affine[0, total] + affine[1, total]
-            a = h + h * jnp.tanh(h)
-            low = raw[j, rows + 1, at_piece(start), :].astype(F32)
-            low = jnp.where((row == length) & bottom, low, 0.0)
-            store(j, i, q + 1, jnp.where(row < length, a, low))
+            a = (h + h * jnp.tanh(h)).astype(BF16)
+            store(j, i, q + 1, a * in_use + raw[j, rows + 1, at_piece(start), :] * border)
 
     def prepare_edge(j):
+        border = flag((length == rows) & bottom)
         for i in range(SLAB // REM):
             start = piece(j, i)
-            high = raw[j, rows, at_piece(start), :].astype(F32)
-            store(j, i, 0, jnp.where(top, high, 0.0))
-            low = raw[j, rows + 1, at_piece(start), :].astype(F32)
-            store(j, i, rows + 1, jnp.where((length == rows) & bottom, low, 0.0))
+            store(j, i, 0, raw[j, rows, at_piece(start), :] * top)
+            store(j, i, rows + 1, raw[j, rows + 1, at_piece(start), :] * border)
 
     def prepare_pair(j, c):
         prepare(j, 2 * c)
@@ -270,11 +324,15 @@
         at = pl.ds(pl.multiple_of(pair * 2 * width, LANES), 2 * width)
         acc[:, at] = total if first else acc[:, at] + total
 
-    def conv(j, pair, first=False):
-        add_to(pair, term(j, pair, 0) + term(j, pair, 1) + term(j, pair, 2), first)
-
-    def conv_rem(g, pair):
-        add_to(pair, term_rem(g, pair, 0) + term_rem(g, pair, 1) + term_rem(g, pair, 2))
+    def products(pair, steps, slabs_in, groups_in):
+        total = None
+        for dy in steps:
+            for j in slabs_in:
+                one = term(j, pair, dy)
+                total = one if total is None else total + one
+            for g in groups_in:
+                total = total + term_rem(g, pair, dy)
+        return total
 
     def wait_weights(j):
         pltpu.make_async_copy(wts.at[:, j], wts.at[:, j], wt_sem.at[j]).wait()
@@ -294,61 +352,99 @@
     st_z[z] = chip_sum
     wait_weights(0)
 
-    @pl.loop(0, pairs // 2)
-    def _(pair):
-        conv(0, pair, first=True)
-
-    for k in range(1, nz):
-        send(st_own.at[2], st_z.at[z], stat_send.at[3 + k], z_recv.at[k - 1], {"strip": to_z(k)})
-
-    @pl.loop(pairs // 2, pairs)
-    def _(pair):
-        conv(0, pair, first=True)
+    for pair in range(pairs // 2):
+        add_to(pair, products(pair, (0, 1, 2), (0,), ()), first=True)
+
+    reach = ((1, nz - 1), (2, nz - 2), tuple(range(3, nz - 2)))
+    if nz < 4:
+        reach = ((1,), (), ())
+
+    def send_z(step):
+        for k in reach[step]:
+            send(
+                st_own.at[2], st_z.at[z], stat_send.at[3 + k], z_recv.at[k - 1],
+                {"strip": to_z(k)},
+            )
+
+    def got_z(step):
+        for k in reach[step]:
+            wait_for(st_z.at[(z + nz - k) % nz], z_recv.at[k - 1])
+
+    send_z(0)
+
+    for pair in range(pairs // 2, pairs):
+        add_to(pair, products(pair, (0, 1, 2), (0,), ()), first=True)
+
+    got_z(0)
+    send_z(1)
 
     def got(c):
         for d in range(2):
             wait_for(pair_of(1 + d, c), own_recv.at[d, c])
 
-    def forward(d, at, first, number):
-        part = pl.ds(first, number)
+    plan = [
+        [(rows + 1 - d, 0, SLAB)]
+        + [(2 * i + d, 0, SLAB) for i in range(pairs - 1)]
+        + [(rows - 2, d * (SLAB // 2), SLAB // 2), (rows - 1, d * (SLAB // 2), SLAB // 2)]
+        for d in range(2)
+    ]
+
+    def forward(d, k):
+        q, start, number = plan[d][k]
+        part = pl.ds(start, number)
         send(
-            raw.at[1 + d, part], raw.at[3, part], fwd_send.at[d, at], fwd_recv.at[d, at],
+            raw.at[1 + d, q, part], raw.at[3, q, part], fwd_send.at[d, k], fwd_recv.at[d, k],
             {"chan": (right, left)[d]},
         )
 
-    def got_far(d, at, first, number):
-        wait_for(raw.at[3, pl.ds(first, number)], fwd_recv.at[d, at])
-
-    plan = (
-        ((rows, 2), (0, 2), (6, 1)),
-        ((2, 2), (4, 2), (7, 1)),
-    )
+    def got_far(k):
+        for d in range(2):
+            q, start, number = plan[d][k]
+            wait_for(raw.at[3, q, pl.ds(start, number)], fwd_recv.at[d, k])
 
     got(0)
     got(1)
-    forward(1, 0, *plan[1][0])
     got(edge)
-    forward(0, 0, *plan[0][0])
-    forward(0, 1, *plan[0][1])
+    for k in range(3):
+        for d in range(2):
+            forward(d, k)
     wait_weights(1)
     wait_weights(2)
+    wait_weights_rem(0)
 
     @pl.loop(1, 3)
     def _(j):
         prepare_edge(j)
         prepare_pair(j, 0)
         prepare_pair(j, 1)
-        conv(j, 0)
-
-    for k in range(1, nz):
-        wait_for(st_z.at[(z + nz - k) % nz], z_recv.at[k - 1])
+
+    def add_sides(pair, *steps):
+        add_to(pair, products(pair, steps, (1, 2), (0,)))
+
+    add_sides(0, 0, 1, 2)
+    add_sides(1, 0, 1)
+    got_z(1)
+    send_z(2)
+    got(2)
+    for d in range(2):
+        forward(d, 3)
+
+    @pl.loop(1, 3)
+    def _(j):
+        prepare_pair(j, 2)
+
+    add_sides(1, 2)
+    add_sides(2, 0, 1)
+    got_z(2)
     line_sum = st_z[0]
     for k in range(1, nz):
         line_sum = line_sum + st_z[k]
     st_own[3] = line_sum
     st_y[y] = line_sum
-    got(2)
-    forward(1, 1, *plan[1][1])
+    got(3)
+    for k in range(4, 6):
+        for d in range(2):
+            forward(d, k)
     for k in range(1, ny):
         send(
             st_own.at[3], st_y.at[y], stat_send.at[2 + nz + k], y_recv.at[k - 1],
@@ -357,41 +453,20 @@
 
     @pl.loop(1, 3)
     def _(j):
-        prepare_pair(j, 2)
-        conv(j, 1)
-
-    got(3)
-    forward(0, 2, *plan[0][2])
-    forward(1, 2, *plan[1][2])
-
-    @pl.loop(1, 3)
-    def _(j):
         prepare_pair(j, 3)
-        conv(j, 2)
-        conv(j, 3)
-
-    wait_weights_rem(0)
-
-    @pl.loop(0, pairs)
-    def _(pair):
-        conv_rem(0, pair)
+
+    add_sides(2, 2)
+    add_sides(3, 0, 1, 2)
 
     for k in range(1, ny):
         wait_for(st_y.at[(y + ny - k) % ny], y_recv.at[k - 1])
     image_sum = st_y[0]
     for k in range(1, ny):
         image_sum = image_sum + st_y[k]
-    moments_out[...] = image_sum / float(strips * (3 * rows // 4) * width * per_group)
+    moments[...] = image_sum / float(strips * (3 * rows // 4) * width * per_group)
 
     wait_weights(3)
     wait_weights_rem(1)
-    got_far(0, 0, *plan[0][0])
-    got_far(1, 0, *plan[1][0])
-    prepare_edge(3)
-    prepare_pair(3, 1)
-    got_far(0, 1, *plan[0][1])
-    got_far(1, 1, *plan[1][1])
-
     outs = []
 
     def finish(pair):
@@ -406,39 +481,56 @@
         copy.start()
         outs.append(copy)
 
-    @pl.loop(0, 2)
-    def _(i):
-        prepare_pair(3, 2 * i)
-
-    @pl.loop(0, 2)
-    def _(pair):
-        conv(3, pair)
-        conv_rem(1, pair)
-
+    def both(pair, *steps):
+        add_to(pair, products(pair, steps, (3,), (1,)))
+
+    got_far(0)
+    prepare_edge(3)
+    got_far(1)
+    prepare_pair(3, 0)
+    both(0, 0, 1)
+    got_far(2)
+    prepare_pair(3, 1)
+    both(0, 2)
     finish(0)
+    both(1, 0, 1)
+    put(0)
+    got_far(3)
+    prepare_pair(3, 2)
+    both(1, 2)
     finish(1)
-    add_to(2, term(3, 2, 0) + term(3, 2, 1) + term_rem(1, 2, 0) + term_rem(1, 2, 1))
-    put(0)
+    both(2, 0, 1)
     put(1)
-    got_far(0, 2, *plan[0][2])
-    got_far(1, 2, *plan[1][2])
-    prepare_pair(3, 3)
-    add_to(2, term(3, 2, 2) + term_rem(1, 2, 2))
+    got_far(4)
+    prepare(3, rows - 2)
+    both(2, 2)
     finish(2)
+    both(3, 0)
     put(2)
-    conv(3, 3)
-    conv_rem(1, 3)
+    got_far(5)
+    prepare(3, rows - 1)
+    both(3, 1, 2)
     finish(3)
     put(3)
 
+    copy = pltpu.make_async_copy(moments, moments_hbm, small_sem.at[7])
+    copy.start()
+    outs.append(copy)
     for copy in sends:
         copy.wait_send()
+    wait_for(edge_hbm.at[0], edge_send.at[1])
+
+    @pl.when(turns)
+    def _():
+        wait_for(hop, edge_send.at[2])
+
     for copy in outs:
         copy.wait()
 
 
 def spread_kernel(
-    rows, width, local, block_hbm, moments, up_hbm, mean_out, square_out, block, buf, in_sem, out_sem
+    rows, width, local, block_hbm, moments_hbm, up_hbm, mean_hbm, square_hbm,
+    block, moments, mean_out, square_out, buf, in_sem, out_sem,
 ):
     takes = []
     for r in range(0, rows, 2):
@@ -446,13 +538,12 @@
         copy = pltpu.make_async_copy(block_hbm.at[at], block.at[at], in_sem.at[r // 2])
         copy.start()
         takes.append(copy)
+    take = pltpu.make_async_copy(moments_hbm, moments, in_sem.at[rows // 2])
+    take.start()
     twice = (
         lax.broadcasted_iota(jnp.int32, (width, 2 * width), 1) // 2
         == lax.broadcasted_iota(jnp.int32, (width, 2 * width), 0)
     ).astype(F32).astype(BF16)
-    groups = mean_out.shape[1]
-    mean_out[...] = moments[0:1, 0:groups]
-    square_out[...] = moments[1:2, 0:groups]
     puts = []
     for r in range(rows):
         if r % 2 == 0:
@@ -462,6 +553,14 @@
             copy = pltpu.make_async_copy(buf.at[r], up_hbm.at[2 * r + a], out_sem.at[2 * r + a])
             copy.start()
             puts.append(copy)
+    groups = mean_out.shape[1]
+    take.wait()
+    mean_out[...] = moments[0:1, 0:groups]
+    square_out[...] = moments[1:2, 0:groups]
+    for i, (src, dst) in enumerate(((mean_out, mean_hbm), (square_out, square_hbm))):
+        copy = pltpu.make_async_copy(src, dst, out_sem.at[2 * rows + i])
+        copy.start()
+        puts.append(copy)
     for copy in puts:
         copy.wait()
 
@@ -482,7 +581,6 @@
 
     dma = pltpu.SemaphoreType.DMA
     any_space = pl.BlockSpec(memory_space=pl.ANY)
-    vmem = pl.BlockSpec(memory_space=pltpu.VMEM)
     smem = pl.BlockSpec(memory_space=pltpu.SMEM)
     flops = 2 * rows * width * 9 * channels * local
     block, moments = pl.pallas_call(
@@ -492,9 +590,19 @@
             jax.ShapeDtypeStruct((rows, local, width), BF16),
             jax.ShapeDtypeStruct((8, LANES), F32),
         ),
-        in_specs=[any_space] * 3 + [vmem] * 3 + [smem] + [vmem] * 4,
-        out_specs=(any_space, vmem),
+        in_specs=[any_space] * 6 + [smem] + [any_space] * 4,
+        out_specs=(any_space, any_space),
         scratch_shapes=[
+            pltpu.VMEM((channels // LANES, LANES), F32),
+            pltpu.VMEM((channels // LANES, LANES), F32),
+            pltpu.VMEM((channels // LANES, LANES), jnp.int32),
+            pltpu.VMEM((1, groups), F32),
+            pltpu.VMEM((1, groups), F32),
+            pltpu.VMEM((1, groups), F32),
+            pltpu.VMEM((1, groups), F32),
+            pltpu.VMEM((8, LANES), F32),
+            dma((8,)),
+            pltpu.VMEM((local, width), BF16),
             pltpu.VMEM((chans, rows + 2, local, width), BF16),
             pltpu.VMEM((chans, 3 * MAIN, (rows + 2) * width), BF16),
             pltpu.VMEM((2, 3 * LANES, (rows + 2) * width), BF16),
@@ -514,10 +622,10 @@
             dma((chans + 2,)),
             dma((2, pairs + 1)),
             dma((2, pairs + 1)),
-            dma((2, 3)),
-            dma((2, 3)),
-            dma((2,)),
-            dma((2,)),
+            dma((2, 6)),
+            dma((2, 6)),
+            dma((3,)),
+            dma((3,)),
             dma((3 + nz + ny,)),
             dma((chans - 1,)),
             dma((1,)),
@@ -545,13 +653,16 @@
             jax.ShapeDtypeStruct((1, groups), F32),
             jax.ShapeDtypeStruct((1, groups), F32),
         ),
-        in_specs=[any_space, vmem],
-        out_specs=(any_space, vmem, vmem),
+        in_specs=[any_space, any_space],
+        out_specs=(any_space, any_space, any_space),
         scratch_shapes=[
             pltpu.VMEM((rows, local, width), BF16),
+            pltpu.VMEM((8, LANES), F32),
+            pltpu.VMEM((1, groups), F32),
+            pltpu.VMEM((1, groups), F32),
             pltpu.VMEM((rows, local, 2 * width), BF16),
-            dma((pairs,)),
-            dma((2 * rows,)),
+            dma((pairs + 1,)),
+            dma((2 * rows + 2,)),
         ],
         compiler_params=pltpu.CompilerParams(vmem_limit_bytes=60 * 1024 * 1024),
     )(block, moments)

time: 48.9 us -> 44.3 us (0.906)
  Pallas kernels: 47.4 us -> 42.5 us
    pallas_call x1, Pallas kernels: 43.4 us -> 39.6 us  [per_device(): pl.pallas_call(functools.partial(main_kernel, rows, width, strips, chans,...]
    pallas_call x1, Pallas kernels: 4.04 us -> 2.9 us  [per_device(): pl.pallas_call(functools.partial(spread_kernel, rows, width, local), name...]
where the time goes in v3:
time: 44.3 us; the launch traced here: 43.8 us
  Pallas kernels  42.5 us (96%)
  between operations  1.29 us (3%)
    pallas_call x1, Pallas kernels, per_device(): pl.pallas_call(functools.partial(main_kernel, rows, width, strips, chans,...  39.6 us
    pallas_call x1, Pallas kernels, per_device(): pl.pallas_call(functools.partial(spread_kernel, rows, width, local), name...  2.9 us

profile of v3, /device:TPU:8, one launch (start us, length us, event | category | flops | bytes accessed | tf_op | source)
XLA Modules:
  0.0 43.8 jit_solution(2106832825907566156)
XLA Ops:
  1.3 39.6 %gather_conv.1 = (bf16[8,320,128]{2,1,0:T(8,128)(2,1)}, f32[8,128]{1,0:T(8,128)}) custom-call(bf16[8,320,128]{2,1,0:T(8,128)(2,1)} %bitcast.13, bf16[2,320,128]{2,1,0:T(8,128)(2,1)} %bitcast.14, bf16[9,320,1280]{2,1,0:T(8,128)(2,1)} %bitcast.11, f32[10,128]{1,0:T(8,128)} %bitcast.15, f32[10,128]{1,0:T(8,128)} %bitcast.16, s32[10,128]{1,0:T(8,128)} %bitcast.17, ...), custom_call_target="tpu_custom_call" | custom-call | flops 7549747200 | bytes 7372800 | tf_op jit(solution)/shard_map/gather_conv/pallas_call | solution.py:586
  40.9 2.9 %spread.1 = (bf16[16,320,256]{2,1,0:T(8,128)(2,1)}, f32[1,32]{1,0:T(1,128)}, f32[1,32]{1,0:T(1,128)}) custom-call(bf16[8,320,128]{2,1,0:T(8,128)(2,1)} %get-tuple-element.8.block_hbm, f32[8,128]{1,0:T(8,128)} %get-tuple-element.9.moments_hbm), custom_call_target="tpu_custom_call" | custom-call | tf_op jit(solution)/shard_map/spread/pallas_call | solution.py:648

commit v4 on v3

--- a/solution.py
+++ b/solution.py
@@ -244,6 +244,11 @@
     var = jnp.maximum(square - mean * mean, 0.5 * (fresh_square - fresh_mean * fresh_mean))
     rstd = lax.rsqrt(var + EPS)
     for t in range(tiles):
+        if t == 2:
+            send(
+                st_own.at[1], st_core.at[core], stat_send.at[3], core_recv.at[0],
+                {"strip": partner},
+            )
         at = slice(t * LANES, (t + 1) * LANES)
         member = group_col[at] == lane
         rstd_c = jnp.sum(jnp.where(member, rstd, 0.0), axis=1, keepdims=True)
@@ -252,9 +257,6 @@
         shift = columns[:, tiles + t:tiles + t + 1] - mean_c * scale
         affine[0, at] = jnp.broadcast_to(0.5 * scale, (LANES, LANES))
         affine[1, at] = jnp.broadcast_to(0.5 * shift, (LANES, LANES))
-    send(
-        st_own.at[1], st_core.at[core], stat_send.at[3], core_recv.at[0], {"strip": partner}
-    )
 
     def flag(condition):
         return jnp.where(condition, 1.0, 0.0).astype(BF16)
@@ -340,20 +342,10 @@
     def wait_weights_rem(g):
         pltpu.make_async_copy(wts_rem.at[:, g], wts_rem.at[:, g], wt_sem.at[chans + g]).wait()
 
-    prepare_edge(0)
-
-    @pl.loop(0, rows)
-    def _(q):
-        prepare(0, q)
-
     wait_for(st_core.at[1 - core], core_recv.at[0])
     chip_sum = st_core[0] + st_core[1]
     st_own[2] = chip_sum
     st_z[z] = chip_sum
-    wait_weights(0)
-
-    for pair in range(pairs // 2):
-        add_to(pair, products(pair, (0, 1, 2), (0,), ()), first=True)
 
     reach = ((1, nz - 1), (2, nz - 2), tuple(range(3, nz - 2)))
     if nz < 4:
@@ -370,13 +362,18 @@
         for k in reach[step]:
             wait_for(st_z.at[(z + nz - k) % nz], z_recv.at[k - 1])
 
+    prepare_edge(0)
     send_z(0)
 
-    for pair in range(pairs // 2, pairs):
+    @pl.loop(0, rows)
+    def _(q):
+        prepare(0, q)
+
+    wait_weights(0)
+
+    for pair in range(pairs):
         add_to(pair, products(pair, (0, 1, 2), (0,), ()), first=True)
 
-    got_z(0)
-    send_z(1)
 
     def got(c):
         for d in range(2):
@@ -408,6 +405,8 @@
     for k in range(3):
         for d in range(2):
             forward(d, k)
+    got_z(0)
+    send_z(1)
     wait_weights(1)
     wait_weights(2)
     wait_weights_rem(0)
@@ -423,8 +422,6 @@
 
     add_sides(0, 0, 1, 2)
     add_sides(1, 0, 1)
-    got_z(1)
-    send_z(2)
     got(2)
     for d in range(2):
         forward(d, 3)
@@ -435,62 +432,57 @@
 
     add_sides(1, 2)
     add_sides(2, 0, 1)
+    got_z(1)
+    send_z(2)
+    got(3)
+    for k in range(4, 6):
+        for d in range(2):
+            forward(d, k)
+    @pl.loop(1, 3)
+    def _(j):
+        prepare_pair(j, 3)
+
+    add_sides(2, 2)
+    add_sides(3, 0, 1, 2)
+
+    wait_weights(3)
+    wait_weights_rem(1)
+    outs = []
+
+    def finish(pair):
+        for h in range(2):
+            r = 2 * pair + h
+            value = raw[0, r].astype(F32) + acc[:, r * width:(r + 1) * width]
+            block[r] = jnp.where(r < length, value, 0.0).astype(BF16)
+
+    def put(pair):
+        at = pl.ds(2 * pair, 2)
+        copy = pltpu.make_async_copy(block.at[at], block_hbm.at[at], out_sem.at[pair])
+        copy.start()
+        outs.append(copy)
+
+    def both(pair, *steps):
+        add_to(pair, products(pair, steps, (3,), (1,)))
+
+    got_far(0)
+    prepare_edge(3)
+    got_far(1)
+    prepare_pair(3, 0)
+    both(0, 0, 1)
     got_z(2)
     line_sum = st_z[0]
     for k in range(1, nz):
         line_sum = line_sum + st_z[k]
     st_own[3] = line_sum
     st_y[y] = line_sum
-    got(3)
-    for k in range(4, 6):
-        for d in range(2):
-            forward(d, k)
+
+    got_far(2)
+    prepare_pair(3, 1)
     for k in range(1, ny):
         send(
             st_own.at[3], st_y.at[y], stat_send.at[2 + nz + k], y_recv.at[k - 1],
             {"strip": to_y(k)},
         )
-
-    @pl.loop(1, 3)
-    def _(j):
-        prepare_pair(j, 3)
-
-    add_sides(2, 2)
-    add_sides(3, 0, 1, 2)
-
-    for k in range(1, ny):
-        wait_for(st_y.at[(y + ny - k) % ny], y_recv.at[k - 1])
-    image_sum = st_y[0]
-    for k in range(1, ny):
-        image_sum = image_sum + st_y[k]
-    moments[...] = image_sum / float(strips * (3 * rows // 4) * width * per_group)
-
-    wait_weights(3)
-    wait_weights_rem(1)
-    outs = []
-
-    def finish(pair):
-        for h in range(2):
-            r = 2 * pair + h
-            value = raw[0, r].astype(F32) + acc[:, r * width:(r + 1) * width]
-            block[r] = jnp.where(r < length, value, 0.0).astype(BF16)
-
-    def put(pair):
-        at = pl.ds(2 * pair, 2)
-        copy = pltpu.make_async_copy(block.at[at], block_hbm.at[at], out_sem.at[pair])
-        copy.start()
-        outs.append(copy)
-
-    def both(pair, *steps):
-        add_to(pair, products(pair, steps, (3,), (1,)))
-
-    got_far(0)
-    prepare_edge(3)
-    got_far(1)
-    prepare_pair(3, 0)
-    both(0, 0, 1)
-    got_far(2)
-    prepare_pair(3, 1)
     both(0, 2)
     finish(0)
     both(1, 0, 1)
@@ -513,6 +505,12 @@
     finish(3)
     put(3)
 
+    for k in range(1, ny):
+        wait_for(st_y.at[(y + ny - k) % ny], y_recv.at[k - 1])
+    image_sum = st_y[0]
+    for k in range(1, ny):
+        image_sum = image_sum + st_y[k]
+    moments[...] = image_sum / float(strips * (3 * rows // 4) * width * per_group)
     copy = pltpu.make_async_copy(moments, moments_hbm, small_sem.at[7])
     copy.start()
     outs.append(copy)

time: 44.3 us -> 41.5 us (0.937)
  Pallas kernels: 42.5 us -> 40.1 us
    pallas_call x1, Pallas kernels: 39.6 us -> 37.2 us  [per_device(): pl.pallas_call(functools.partial(main_kernel, rows, width, strips, chans,...]
where the time goes in v4:
time: 41.5 us; the launch traced here: 41.4 us
  Pallas kernels  40.1 us (97%)
  between operations  1.29 us (3%)
    pallas_call x1, Pallas kernels, per_device(): pl.pallas_call(functools.partial(main_kernel, rows, width, strips, chans,...  37.2 us
    pallas_call x1, Pallas kernels, per_device(): pl.pallas_call(functools.partial(spread_kernel, rows, width, local), name...  2.91 us

profile of v4, /device:TPU:8, one launch (start us, length us, event | category | flops | bytes accessed | tf_op | source)
XLA Modules:
  0.0 41.4 jit_solution(4492119401374793979)
XLA Ops:
  1.3 37.2 %gather_conv.1 = (bf16[8,320,128]{2,1,0:T(8,128)(2,1)}, f32[8,128]{1,0:T(8,128)}) custom-call(bf16[8,320,128]{2,1,0:T(8,128)(2,1)} %bitcast.13, bf16[2,320,128]{2,1,0:T(8,128)(2,1)} %bitcast.14, bf16[9,320,1280]{2,1,0:T(8,128)(2,1)} %bitcast.11, f32[10,128]{1,0:T(8,128)} %bitcast.15, f32[10,128]{1,0:T(8,128)} %bitcast.16, s32[10,128]{1,0:T(8,128)} %bitcast.17, ...), custom_call_target="tpu_custom_call" | custom-call | flops 7549747200 | bytes 7372800 | tf_op jit(solution)/shard_map/gather_conv/pallas_call | solution.py:584
  38.5 2.9 %spread.1 = (bf16[16,320,256]{2,1,0:T(8,128)(2,1)}, f32[1,32]{1,0:T(1,128)}, f32[1,32]{1,0:T(1,128)}) custom-call(bf16[8,320,128]{2,1,0:T(8,128)(2,1)} %get-tuple-element.8.block_hbm, f32[8,128]{1,0:T(8,128)} %get-tuple-element.9.moments_hbm), custom_call_target="tpu_custom_call" | custom-call | tf_op jit(solution)/shard_map/spread/pallas_call | solution.py:646

commit v5 on v4

--- a/solution.py
+++ b/solution.py
@@ -317,23 +317,23 @@
     def term(j, pair, dy):
         return jnp.dot(wts[dy, j], feats[j, :, cells_of(pair, dy)], preferred_element_type=F32)
 
-    def term_rem(g, pair, dy):
-        return jnp.dot(
-            wts_rem[dy, g], feats_rem[g, :, cells_of(pair, dy)], preferred_element_type=F32
-        )
-
     def add_to(pair, total, first=False):
         at = pl.ds(pl.multiple_of(pair * 2 * width, LANES), 2 * width)
         acc[:, at] = total if first else acc[:, at] + total
 
+    def term_rems(g, pair, steps):
+        left_side = jnp.concatenate([wts_rem[dy, g] for dy in steps], axis=1)
+        patch = jnp.concatenate([feats_rem[g, :, cells_of(pair, dy)] for dy in steps], axis=0)
+        return jnp.dot(left_side, patch, preferred_element_type=F32)
+
     def products(pair, steps, slabs_in, groups_in):
         total = None
-        for dy in steps:
-            for j in slabs_in:
+        for j in slabs_in:
+            for dy in steps:
                 one = term(j, pair, dy)
                 total = one if total is None else total + one
-            for g in groups_in:
-                total = total + term_rem(g, pair, dy)
+        for g in groups_in:
+            total = total + term_rems(g, pair, steps)
         return total
 
     def wait_weights(j):
@@ -411,8 +411,7 @@
     wait_weights(2)
     wait_weights_rem(0)
 
-    @pl.loop(1, 3)
-    def _(j):
+    for j in (1, 2):
         prepare_edge(j)
         prepare_pair(j, 0)
         prepare_pair(j, 1)
@@ -426,8 +425,7 @@
     for d in range(2):
         forward(d, 3)
 
-    @pl.loop(1, 3)
-    def _(j):
+    for j in (1, 2):
         prepare_pair(j, 2)
 
     add_sides(1, 2)
@@ -438,8 +436,7 @@
     for k in range(4, 6):
         for d in range(2):
             forward(d, k)
-    @pl.loop(1, 3)
-    def _(j):
+    for j in (1, 2):
         prepare_pair(j, 3)
 
     add_sides(2, 2)

time: 41.5 us -> 41.1 us (level)
  Pallas kernels: 40.1 us -> 39.5 us
    pallas_call x1, Pallas kernels: 37.2 us -> 36.7 us  [per_device(): pl.pallas_call(functools.partial(main_kernel, rows, width, strips, chans,...]
where the time goes in v5:
time: 41.1 us; the launch traced here: 40.8 us
  Pallas kernels  39.5 us (96%)
  between operations  1.29 us (3%)
    pallas_call x1, Pallas kernels, per_device(): pl.pallas_call(functools.partial(main_kernel, rows, width, strips, chans,...  36.7 us
    pallas_call x1, Pallas kernels, per_device(): pl.pallas_call(functools.partial(spread_kernel, rows, width, local), name...  2.89 us

profile of v5, /device:TPU:8, one launch (start us, length us, event | category | flops | bytes accessed | tf_op | source)
XLA Modules:
  0.0 40.8 jit_solution(9987651725951030550)
XLA Ops:
  1.3 36.7 %gather_conv.1 = (bf16[8,320,128]{2,1,0:T(8,128)(2,1)}, f32[8,128]{1,0:T(8,128)}) custom-call(bf16[8,320,128]{2,1,0:T(8,128)(2,1)} %bitcast.13, bf16[2,320,128]{2,1,0:T(8,128)(2,1)} %bitcast.14, bf16[9,320,1280]{2,1,0:T(8,128)(2,1)} %bitcast.11, f32[10,128]{1,0:T(8,128)} %bitcast.15, f32[10,128]{1,0:T(8,128)} %bitcast.16, s32[10,128]{1,0:T(8,128)} %bitcast.17, ...), custom_call_target="tpu_custom_call" | custom-call | flops 7549747200 | bytes 7372800 | tf_op jit(solution)/shard_map/gather_conv/pallas_call | solution.py:581
  37.9 2.9 %spread.1 = (bf16[16,320,256]{2,1,0:T(8,128)(2,1)}, f32[1,32]{1,0:T(1,128)}, f32[1,32]{1,0:T(1,128)}) custom-call(bf16[8,320,128]{2,1,0:T(8,128)(2,1)} %get-tuple-element.8.block_hbm, f32[8,128]{1,0:T(8,128)} %get-tuple-element.9.moments_hbm), custom_call_target="tpu_custom_call" | custom-call | tf_op jit(solution)/shard_map/spread/pallas_call | solution.py:643
